TPU v7x, 32 devices: a whole 2x2x4 slice. The times are simulated.
32 devices in a mesh: dp: 4 (over z), tp: 8 (over y, x, core).
Axes of the slice: x: 2, y: 2, z: 4, core: 2. Of those that a mesh axis runs over, the one named last changes fastest.
Arguments:
- hidden: bfloat16 [512, 1536], P('dp'), parts along dimension 0
- tokens: int32 [512], P('dp'), parts along dimension 0
- embedding: bfloat16 [151936, 1536], P('tp')
- head_w: bfloat16 [1536, 151936], P(None, 'tp')
- h_norm: float32 [1536], replicated
- e_norm: float32 [1536], replicated
- f_norm: float32 [1536], replicated
- o_norm: float32 [1536], replicated
- proj_w: bfloat16 [3072, 1536], P(None, 'tp')
- w_gate: bfloat16 [1536, 8960], P(None, 'tp')
- w_up: bfloat16 [1536, 8960], P(None, 'tp')
- w_down: bfloat16 [8960, 1536], P('tp')
Outputs:
- output 1: bfloat16 [512, 1536], P('dp'), parts along dimension 0
- output 2: float32 [512, 151936], P('dp', 'tp'), parts along dimension 0
There are 4 independent parts. A program takes and returns all parts, laid end to end along the dimension named above; an argument that names none is the same for every part.
All inputs are finite; a program needn't handle non-finite values.
Results may differ from a plain program's by a relative error of at most 0.0111825.
Values are sent between devices in bfloat16 or wider.
A program may use at most 1 GiB of HBM per device.

v0:
```python
import jax
import jax.numpy as jnp
from jax import lax
from jax.sharding import PartitionSpec as P

NORM_EPS = 1e-6


def rms_norm(values, norm_gain):
    wide_vals = values.astype(jnp.float32)
    inv_rms = lax.rsqrt(jnp.mean(wide_vals * wide_vals, axis=-1, keepdims=True) + NORM_EPS)
    return wide_vals * inv_rms * norm_gain


def solution(mesh):
    def draft_step(hidden, tokens, embedding, head_w, h_norm, e_norm, f_norm, o_norm, proj_w, w_gate, w_up, w_down):
        tp_index = lax.axis_index("tp")
        vocab_local = embedding.shape[0]
        local_ids = tokens - tp_index * vocab_local
        owned_mask = (local_ids >= 0) & (local_ids < vocab_local)
        picked = jnp.take(embedding, jnp.clip(local_ids, 0, vocab_local - 1), axis=0)
        picked = jnp.where(owned_mask[:, None], picked, jnp.zeros_like(picked))
        emb_rows = lax.psum(picked, "tp")
        joined = jnp.concatenate([rms_norm(hidden, h_norm), rms_norm(emb_rows, e_norm)], axis=-1).astype(jnp.bfloat16)
        proj_cols = jnp.dot(joined, proj_w, preferred_element_type=jnp.float32).astype(jnp.bfloat16)
        proj_full = lax.all_gather(proj_cols, "tp", axis=1, tiled=True)
        normed = rms_norm(proj_full, f_norm).astype(jnp.bfloat16)
        gate_val = jnp.dot(normed, w_gate, preferred_element_type=jnp.float32)
        up_val = jnp.dot(normed, w_up, preferred_element_type=jnp.float32)
        act_val = (jax.nn.silu(gate_val) * up_val).astype(jnp.bfloat16)
        down_part = jnp.dot(act_val, w_down, preferred_element_type=jnp.float32)
        down_sum = lax.psum(down_part, "tp")
        new_u = (proj_full.astype(jnp.float32) + down_sum).astype(jnp.bfloat16)
        out_norm = rms_norm(new_u, o_norm).astype(jnp.bfloat16)
        logits = jnp.dot(out_norm, head_w, preferred_element_type=jnp.float32)
        row_max = lax.pmax(jnp.max(logits, axis=-1), "tp")
        shifted = logits - row_max[:, None]
        row_sum = lax.psum(jnp.sum(jnp.exp(shifted), axis=-1), "tp")
        return new_u, shifted - jnp.log(row_sum)[:, None]

    specs_in = (P("dp", None), P("dp"), P("tp", None), P(None, "tp"), P(None), P(None), P(None), P(None), P(None, "tp"), P(None, "tp"), P(None, "tp"), P("tp", None))
    specs_out = (P("dp", None), P("dp", "tp"))
    return jax.shard_map(draft_step, mesh=mesh, in_specs=specs_in, out_specs=specs_out, check_vma=False)
```

profile of v0, /device:TPU:0, one launch (start us, length us, event | category | flops | bytes accessed | tf_op | source)
XLA Modules:
  0.0 232.3 jit_solution(13673738577264258312)
XLA Ops:
  7.2 0.0 copy-start
  7.2 0.0 copy-start.3
  7.2 0.0 copy-start.4
  7.2 0.0 all-reduce.3.cloned.1.call-start
  7.3 0.8 compare_and_fusion
  8.1 11.6 %gather_fusion = bf16[128,1536]{1,0:T(8,128)(2,1)} fusion(bf16[18992,1536]{1,0:T(8,128)(2,1)} %param.14, s32[1024]{0:T(1024)S(1)} %pad_clamp_fusion), kind=kCustom, calls=%fused_computation | custom fusion | bytes 786944 | tf_op jit(solution)/shard_map/jit(_take)/gather | solution.py:21
  19.7 0.0 copy-start.6
  19.7 1.9 select_select_fusion
  21.6 0.0 all-reduce.3.cloned.1.call-update
  21.6 0.0 all-reduce.5.cloned.1.call-start
  21.7 1.2 fusion.2
  22.8 0.0 copy-done.3
  22.8 1.9 fusion.4
  24.7 51.9 %all-reduce.3.cloned.1.call-done = bf16[128,1536]{1,0:T(8,128)(2,1)} async-done(((bf16[128,1536]{1,0:T(8,128)(2,1)}), bf16[128,1536]{1,0:T(8,128)(2,1)}) %all-reduce.3.cloned.1.call-update) | async-done | bytes 393232 | tf_op jit(solution)/shard_map/psum | solution.py:23
  76.6 0.0 copy-start.5
  76.6 1.3 fusion.5
  77.9 0.0 copy-done.4
  77.9 1.2 fusion.7
  79.1 1.9 convolution_convert_fusion
  81.0 9.0 %all_gather.3 = bf16[128,1536]{0,1:T(8,128)(2,1)S(1)} all-gather(bf16[128,192]{0,1:T(8,128)(2,1)S(1)} %convolution_convert_fusion), channel_id=1, replica_groups=mesh['dp'=4,'tp'=8] {'tp'}, dimensions={1}, use_global_device_ids=true | all-gather | bytes 442368 | tf_op jit(solution)/shard_map/all_gather | solution.py:26
  90.0 0.0 copy-start.2
  90.0 0.2 fusion.11
  90.3 0.5 copy-done.2
  90.8 0.0 copy-done.6
  90.8 0.0 copy-done.5
  90.8 2.0 fusion.28
  92.8 0.0 copy-done
  92.8 0.0 copy-start.7
  92.8 6.8 %fusion.1 = f32[128,1536]{0,1:T(8,128)} fusion(bf16[1120,1536]{1,0:T(8,128)(2,1)S(1)} %copy-done, bf16[1536,1120]{0,1:T(8,128)(2,1)} %param.22, f32[128,1120]{0,1:T(8,128)} %fusion.28, bf16[128,1536]{0,1:T(8,128)(2,1)} %copy-done.2, f32[1536]{0:T(1024)S(1)} %copy-done.6, f32[128]{0:T(128)S(1)} %add_rsqrt_fusion.1), kind=kOutput, calls=%fused_computation.9 | convolution fusion | flops 882450432 | bytes 8641024 | tf_op jit(solution)/shard_map/dot_general | solution.py:31
  99.6 0.0 all-reduce.5.cloned.1.call-update
  99.6 55.3 %all-reduce.5.cloned.1.call-done = f32[128,1536]{0,1:T(8,128)} async-done(((f32[128,1536]{0,1:T(8,128)}), f32[128,1536]{0,1:T(8,128)}) %all-reduce.5.cloned.1.call-update) | async-done | bytes 786448 | tf_op jit(solution)/shard_map/psum | solution.py:32
  154.9 1.5 fusion.8
  156.4 0.9 copy.15
  157.3 0.0 copy-done.7
  157.3 30.3 %fusion.35 = (f32[128]{0:T(128)S(1)}, f32[128,18992]{0,1:T(8,128)}) fusion(bf16[1536,18992]{0,1:T(8,128)(2,1)} %param.15, bf16[128,1536]{0,1:T(8,128)(2,1)S(1)} %get-tuple-element.5, f32[1536]{0:T(1024)S(1)} %copy-done.7, f32[128]{0:T(128)S(1)} %add_rsqrt_fusion), kind=kOutput, calls=%fused_computation.53 | convolution fusion | flops 7471175680 | bytes 68467712 | tf_op jit(solution)/shard_map/dot_general | solution.py:35
  187.6 11.8 %pmax.7 = f32[128]{0:T(128)S(1)} all-reduce(f32[128]{0:T(128)S(1)} %get-tuple-element.9), channel_id=1, replica_groups=mesh['dp'=4,'tp'=8] {'tp'}, use_global_device_ids=true, to_apply=%region_7.8 | all-reduce | flops 128 | bytes 1024 | tf_op jit(solution)/shard_map/pmax | solution.py:36
  199.4 5.6 %exponential_reduce_fusion = f32[128]{0:T(128)S(1)} fusion(f32[128,18992]{0,1:T(8,128)} %get-tuple-element.10, f32[128]{0:T(128)S(1)} %pmax.7), kind=kLoop, calls=%fused_computation.1 | loop fusion | flops 4861824 | bytes 9724928 | tf_op jit(solution)/shard_map/reduce_sum | solution.py:38
  204.9 11.8 %psum.23 = f32[128]{0:T(128)S(1)} all-reduce(f32[128]{0:T(128)S(1)} %exponential_reduce_fusion), channel_id=1, replica_groups=mesh['dp'=4,'tp'=8] {'tp'}, use_global_device_ids=true, to_apply=%region_9.10 | all-reduce | flops 128 | bytes 1024 | tf_op jit(solution)/shard_map/psum | solution.py:38
  216.7 0.0 copy-start.1
  216.8 8.7 %subtract_subtract_fusion = f32[128,18992]{0,1:T(8,128)} fusion(f32[128,18992]{0,1:T(8,128)} %get-tuple-element.10, f32[128]{0:T(128)S(1)} %log.3, f32[128]{0:T(128)S(1)} %pmax.7), kind=kLoop, calls=%fused_computation.2 | loop fusion | flops 4861952 | bytes 19448832 | tf_op jit(solution)/shard_map/sub | solution.py:39
  225.5 0.0 copy-done.1
  (6 shorter events, 0.0 us)
Async XLA Ops:
  7.2 85.6 %copy-start = (bf16[1120,1536]{1,0:T(8,128)(2,1)S(1)}, bf16[1120,1536]{1,0:T(8,128)(2,1)}, u32[]{:S(2)}) copy-start(bf16[1120,1536]{1,0:T(8,128)(2,1)} %param.23) | copy-start | bytes 10321924
  7.2 15.6 %copy-start.3 = (f32[1536]{0:T(1024)S(1)}, f32[1536]{0:T(1024)}, u32[]{:S(2)}) copy-start(f32[1536]{0:T(1024)} %param.16) | copy-start | bytes 18436
  7.2 70.8 %copy-start.4 = (f32[1536]{0:T(1024)S(1)}, f32[1536]{0:T(1024)}, u32[]{:S(2)}) copy-start(f32[1536]{0:T(1024)} %param.17) | copy-start | bytes 18436
  7.2 69.4 %all-reduce.3.cloned.1.call-start = ((), (), s32[]{:S(2)}) async-start(), calls=%async_computation | async-start | bytes 786432 | tf_op jit(solution)/shard_map/psum | solution.py:23
  19.7 71.1 %copy-start.6 = (f32[1536]{0:T(1024)S(1)}, f32[1536]{0:T(1024)}, u32[]{:S(2)}) copy-start(f32[1536]{0:T(1024)} %param.18) | copy-start | bytes 18436
  21.6 133.3 %all-reduce.5.cloned.1.call-start = ((), (), s32[]{:S(2)}) async-start(), calls=%async_computation.1 | async-start | bytes 1572864 | tf_op jit(solution)/shard_map/psum | solution.py:32
  76.6 14.2 %copy-start.5 = (bf16[1536,1120]{0,1:T(8,128)(2,1)S(1)}, bf16[1536,1120]{0,1:T(8,128)(2,1)}, u32[]{:S(2)}) copy-start(bf16[1536,1120]{0,1:T(8,128)(2,1)} %param.21) | copy-start | bytes 10321924
  90.0 0.7 copy-start.2
  92.8 64.5 %copy-start.7 = (f32[1536]{0:T(1024)S(1)}, f32[1536]{0:T(1024)}, u32[]{:S(2)}) copy-start(f32[1536]{0:T(1024)} %param.19) | copy-start | bytes 18436
  216.7 8.7 %copy-start.1 = (bf16[1120,1536]{1,0:T(8,128)(2,1)S(1)}, bf16[1120,1536]{1,0:T(8,128)(2,1)}, u32[]{:S(2)}) copy-start(bf16[1120,1536]{1,0:T(8,128)(2,1)} %param.23) | copy-start | bytes 10321924
Sparse Core Ops, SparseCore 0:
  21.7 54.8 all-reduce.2
  99.7 55.1 all-reduce.4
where the time goes:
time: 233 us; the launch traced here: 232 us
  waiting for transfers between devices  107 us (46%)
  matrix products  41 us (18%)
  blocking collectives  32.6 us (14%)
  other arithmetic  24.2 us (10%)
  between operations  14.1 us (6%)
  local copies, waits for them, and re-layouts  13.1 us (6%)
    psum x1, waiting for transfers between devices, draft_step(): down_sum = lax.psum(down_part, 'tp')  55.3 us
    psum x1, waiting for transfers between devices, draft_step(): emb_rows = lax.psum(picked, 'tp')  51.9 us
    dot_general x1, matrix products, draft_step(): logits = jnp.dot(out_norm, head_w, preferred_element_type=jnp.float32)  30.3 us
    psum x1, blocking collectives, draft_step(): row_sum = lax.psum(jnp.sum(jnp.exp(shifted), axis=-1), 'tp')  11.8 us
    pmax x1, blocking collectives, draft_step(): row_max = lax.pmax(jnp.max(logits, axis=-1), 'tp')  11.8 us
    gather x1, local copies, waits for them, and re-layouts, draft_step(): jnp.take(embedding, jnp.clip(local_ids, 0, vocab_local - 1), axis=0)  11.6 us
    all_gather x1, blocking collectives, draft_step(): proj_full = lax.all_gather(proj_cols, 'tp', axis=1, tiled=True)  9.05 us
    sub x1, other arithmetic, draft_step(): return (new_u, shifted - jnp.log(row_sum)[:, None])  8.7 us
  transfers between devices with their start and end apart: 2, of which 2 were waited for; matrix products, arithmetic and copies ran while one was open for 1% of the time, Pallas kernels for 0%

commit v1 on v0

v1 whole, which is shorter than its diff:
```python
import functools

import jax
import jax.numpy as jnp
from jax import lax
from jax.experimental import pallas as pl
from jax.experimental.pallas import tpu as pltpu
from jax.sharding import PartitionSpec as P

NORM_EPS = 1e-6
TILE = 512
SLOTS = 23
MESH = pl.DeviceIdType.MESH
F32, BF16 = jnp.float32, jnp.bfloat16


def rms(values, gain, axis):
    wide = values.astype(F32)
    inv = lax.rsqrt(jnp.mean(wide * wide, axis=axis, keepdims=True) + NORM_EPS)
    return wide * inv * gain


def dot_t(a, b):
    return lax.dot_general(a, b, (((1,), (1,)), ((), ())), preferred_element_type=F32)


def gather_kernel(ids_ref, ids_row_ref, emb_ref, out_ref, buf, sem):
    rows, vocab = out_ref.shape[0], emb_ref.shape[0]
    base = lax.axis_index("tp") * vocab

    def issue(r, carry):
        local = jnp.clip(ids_ref[r] - base, 0, vocab - 1)
        start = pl.multiple_of((local // 8) * 8, 8)
        pltpu.make_async_copy(emb_ref.at[pl.ds(start, 8), :], buf.at[pl.ds(pl.multiple_of(r * 8, 8), 8), :], sem).start()
        return carry

    lax.fori_loop(0, rows, issue, 0, unroll=8)
    local = ids_row_ref[...] - base
    owned = (local >= 0) & (local < vocab)
    want = lax.broadcasted_iota(jnp.int32, (rows * 8, rows), 1) * 8 + (local & 7)
    here = lax.broadcasted_iota(jnp.int32, (rows * 8, rows), 0)
    pick = jnp.where((here == want) & owned, 1.0, 0.0).astype(BF16)
    pltpu.make_async_copy(emb_ref.at[pl.ds(0, rows * 8), :], buf, sem).wait()
    out_ref[...] = lax.dot_general(pick, buf[...], (((0,), (0,)), ((), ())), preferred_element_type=F32).astype(BF16)


def main_kernel(n, hidden_ref, emb_ref, h_gain, e_gain, f_gain, o_gain,
                proj_hbm, gate_hbm, up_hbm, down_hbm, head_hbm,
                z_ref, lse_ref, u_ref,
                proj_v, gate_v, up_v, down_v, ring, emb_in, emb_mine, emb_all, p_mine, p_all,
                part_v, part_in, u_mine, u_all, o_v, stat_mine, stat_in, f_wide, o_wide, m_v, s_v,
                w_sem, ring_sem, send_sem, recv_sem):
    me = lax.axis_index("tp")
    rows, dim = hidden_ref.shape
    chunk = rows // n
    cols = p_mine.shape[0]
    vocab = head_hbm.shape[0]
    tiles = vocab // TILE
    rest = vocab - tiles * TILE

    weights = [pltpu.make_async_copy(src, dst, w_sem.at[i]) for i, (src, dst) in enumerate(
        ((proj_hbm, proj_v), (gate_hbm, gate_v), (up_hbm, up_v), (down_hbm, down_v)))]
    for copy in weights:
        copy.start()

    def head_copy(t):
        slot = lax.rem(t, SLOTS)
        start = pl.multiple_of(t * TILE, TILE)
        return pltpu.make_async_copy(head_hbm.at[pl.ds(start, TILE), :], ring.at[slot], ring_sem.at[slot])

    barrier = pltpu.get_barrier_semaphore()
    for d in range(1, n):
        pl.semaphore_signal(barrier, inc=1, device_id={"tp": lax.rem(me + d, n)}, device_id_type=MESH)
    pl.semaphore_wait(barrier, n - 1)

    def exchange(phase, source, target):
        copies = []
        for d in range(1, n):
            peer = lax.rem(me + d, n)
            copies.append(pltpu.make_async_remote_copy(
                src_ref=source(peer), dst_ref=target(d), send_sem=send_sem.at[phase, d - 1],
                recv_sem=recv_sem.at[phase, d - 1], device_id={"tp": peer}, device_id_type=MESH))
        for copy in copies:
            copy.start()
        return copies

    def part(ref, j, size):
        return ref.at[pl.ds(pl.multiple_of(j * size, size), size), :]

    first = exchange(0, lambda j: part(emb_ref, j, chunk), lambda d: emb_in.at[d - 1])

    def prefetch(t, carry):
        head_copy(t).start()
        return carry

    lax.fori_loop(0, SLOTS, prefetch, 0)

    normed_h = rms(hidden_ref[...], h_gain[...], -1).astype(BF16)
    weights[0].wait()
    acc_h = dot_t(proj_v[:, :dim], normed_h)
    f_wide[...] = jnp.transpose(jnp.broadcast_to(f_gain[...], (rows, dim)))
    o_wide[...] = jnp.transpose(jnp.broadcast_to(o_gain[...], (rows, dim)))
    total = part(emb_ref, me, chunk)[...].astype(F32)
    for d in range(1, n):
        first[d - 1].wait_recv()
        total = total + emb_in[d - 1].astype(F32)
    emb_mine[...] = rms(total, e_gain[...], -1).astype(BF16)
    second = exchange(1, lambda j: emb_mine, lambda d: part(emb_all, me, chunk))
    part(emb_all, me, chunk)[...] = emb_mine[...]
    for copy in second:
        copy.wait_recv()
    p_mine[...] = (acc_h + dot_t(proj_v[:, dim:], emb_all[...])).astype(BF16)

    third = exchange(2, lambda j: p_mine, lambda d: part(p_all, me, cols))
    part(p_all, me, cols)[...] = p_mine[...]
    for copy in third:
        copy.wait_recv()
    normed = rms(p_all[...], f_wide[...], 0).astype(BF16)
    weights[1].wait()
    gate = jnp.dot(gate_v[...], normed, preferred_element_type=F32)
    weights[2].wait()
    up = jnp.dot(up_v[...], normed, preferred_element_type=F32)
    act = (jax.nn.silu(gate) * up).astype(BF16)
    weights[3].wait()
    down = lax.dot_general(act, down_v[...], (((0,), (0,)), ((), ())), preferred_element_type=F32)
    part_v[...] = jnp.transpose(down)

    fourth = exchange(3, lambda j: part(part_v, j, cols), lambda d: part_in.at[d - 1])
    total = part(part_v, me, cols)[...]
    for d in range(1, n):
        fourth[d - 1].wait_recv()
        total = total + part_in[d - 1]
    u_mine[...] = (p_mine[...].astype(F32) + total).astype(BF16)
    fifth = exchange(4, lambda j: u_mine, lambda d: part(u_all, me, cols))
    part(u_all, me, cols)[...] = u_mine[...]
    for copy in fifth:
        copy.wait_recv()
    o_v[...] = rms(u_all[...], o_wide[...], 0).astype(BF16)
    u_ref[...] = u_all[...]

    m_v[...] = jnp.full_like(m_v, -jnp.inf)
    s_v[...] = jnp.zeros_like(s_v)

    def fold(block):
        groups = block.reshape(block.shape[0] // 8, 8, rows)
        old = m_v[...]
        new = jnp.maximum(old, jnp.max(groups, axis=0))
        s_v[...] = s_v[...] * jnp.exp(old - new) + jnp.sum(jnp.exp(groups - new[None]), axis=0)
        m_v[...] = new

    def tile(t, carry):
        head_copy(t).wait()
        block = jnp.dot(ring[lax.rem(t, SLOTS)], o_v[...], preferred_element_type=F32)
        z_ref[pl.ds(pl.multiple_of(t * TILE, TILE), TILE), :] = block
        fold(block)

        @pl.when(t + SLOTS < tiles)
        def _():
            head_copy(t + SLOTS).start()

        @pl.when(t + SLOTS == tiles)
        def _():
            tail_copy().start()
        return carry

    def tail_copy():
        slot = tiles % SLOTS
        return pltpu.make_async_copy(head_hbm.at[pl.ds(tiles * TILE, rest), :], ring.at[slot, pl.ds(0, rest), :], ring_sem.at[slot])

    lax.fori_loop(0, tiles, tile, 0)
    tail_copy().wait()
    block = jnp.dot(ring[tiles % SLOTS, :rest, :], o_v[...], preferred_element_type=F32)
    z_ref[tiles * TILE:, :] = block
    fold(block)

    m_row = jnp.max(m_v[...], axis=0, keepdims=True)
    s_row = jnp.sum(s_v[...] * jnp.exp(m_v[...] - m_row), axis=0, keepdims=True)
    stat_mine[...] = jnp.concatenate([m_row, s_row, jnp.zeros((6, rows), F32)], axis=0)
    sixth = exchange(5, lambda j: stat_mine, lambda d: stat_in.at[me])
    stat_in[me] = stat_mine[...]
    for copy in sixth:
        copy.wait_recv()
    stats = stat_in[...]
    m_all, s_all = stats[:, 0, :], stats[:, 1, :]
    m_top = jnp.max(m_all, axis=0, keepdims=True)
    lse = m_top + jnp.log(jnp.sum(s_all * jnp.exp(m_all - m_top), axis=0, keepdims=True))
    lse_ref[...] = jnp.broadcast_to(lse, lse_ref.shape)
    for group in (first, second, third, fourth, fifth, sixth):
        for copy in group:
            copy.wait_send()


def close_kernel(z_ref, lse_ref, u_in, out_ref, u_out):
    depth, vocab = out_ref.shape[0], z_ref.shape[0]
    i, full = pl.program_id(0), vocab // depth
    rest = vocab - full * depth

    @pl.when(i < full)
    def _():
        out_ref[...] = z_ref[pl.ds(pl.multiple_of(i * depth, depth), depth), :] - lse_ref[0:1, :]

    @pl.when(i == full)
    def _():
        out_ref[:rest, :] = z_ref[full * depth:, :] - lse_ref[0:1, :]

    @pl.when(i == 0)
    def _():
        u_out[...] = jnp.transpose(u_in[...])


def solution(mesh):
    n = mesh.shape["tp"]

    def draft_step(hidden, tokens, embedding, head_w, h_norm, e_norm, f_norm, o_norm, proj_w, w_gate, w_up, w_down):
        rows, dim = hidden.shape
        vocab = head_w.shape[1]
        cols, ffn = proj_w.shape[1], w_gate.shape[1]
        chunk = rows // n
        smem = pl.BlockSpec(memory_space=pltpu.SMEM)
        vmem = pl.BlockSpec(memory_space=pltpu.VMEM)
        hbm = pl.BlockSpec(memory_space=pl.ANY)
        emb_rows = pl.pallas_call(
            gather_kernel,
            out_shape=jax.ShapeDtypeStruct((rows, dim), BF16),
            in_specs=[smem, vmem, hbm],
            out_specs=vmem,
            scratch_shapes=[pltpu.VMEM((rows * 8, dim), BF16), pltpu.SemaphoreType.DMA],
            name="gather_rows",
        )(tokens, tokens[None, :], embedding)

        dma, sem2 = pltpu.SemaphoreType.DMA, (6, n - 1)
        z, lse, u = pl.pallas_call(
            functools.partial(main_kernel, n),
            out_shape=(pltpu.VMEM((vocab, rows), F32), pltpu.VMEM((8, rows), F32), pltpu.VMEM((dim, rows), BF16)),
            in_specs=[vmem] * 6 + [hbm] * 5,
            out_specs=(vmem, vmem, vmem),
            scratch_shapes=[
                pltpu.VMEM((cols, 2 * dim), BF16), pltpu.VMEM((ffn, dim), BF16), pltpu.VMEM((ffn, dim), BF16),
                pltpu.VMEM((ffn, dim), BF16), pltpu.VMEM((SLOTS, TILE, dim), BF16),
                pltpu.VMEM((n - 1, chunk, dim), BF16), pltpu.VMEM((chunk, dim), BF16), pltpu.VMEM((rows, dim), BF16),
                pltpu.VMEM((cols, rows), BF16), pltpu.VMEM((dim, rows), BF16),
                pltpu.VMEM((dim, rows), F32), pltpu.VMEM((n - 1, cols, rows), F32),
                pltpu.VMEM((cols, rows), BF16), pltpu.VMEM((dim, rows), BF16), pltpu.VMEM((dim, rows), BF16),
                pltpu.VMEM((8, rows), F32), pltpu.VMEM((n, 8, rows), F32),
                pltpu.VMEM((dim, rows), F32), pltpu.VMEM((dim, rows), F32),
                pltpu.VMEM((8, rows), F32), pltpu.VMEM((8, rows), F32),
                dma((4,)), dma((SLOTS,)), dma(sem2), dma(sem2),
            ],
            compiler_params=pltpu.CompilerParams(
                collective_id=0, has_side_effects=True, vmem_limit_bytes=53 * 1024 * 1024),
            name="draft_main",
        )(hidden, emb_rows, h_norm[None], e_norm[None], f_norm[None], o_norm[None],
          proj_w.T, w_gate.T, w_up.T, w_down, head_w.T)

        depth = 1920
        logp, new_u = pl.pallas_call(
            close_kernel,
            grid=(pl.cdiv(vocab, depth),),
            out_shape=(jax.ShapeDtypeStruct((vocab, rows), F32), jax.ShapeDtypeStruct((rows, dim), BF16)),
            in_specs=[vmem, vmem, vmem],
            out_specs=(pl.BlockSpec((depth, rows), lambda i: (i, 0)), pl.BlockSpec((rows, dim), lambda i: (0, 0))),
            compiler_params=pltpu.CompilerParams(vmem_limit_bytes=16 * 1024 * 1024),
            name="close",
        )(z, lse, u)
        return new_u, logp.T

    specs_in = (P("dp", None), P("dp"), P("tp", None), P(None, "tp"), P(None), P(None), P(None), P(None), P(None, "tp"), P(None, "tp"), P(None, "tp"), P("tp", None))
    specs_out = (P("dp", None), P("dp", "tp"))
    return jax.shard_map(draft_step, mesh=mesh, in_specs=specs_in, out_specs=specs_out, check_vma=False)
```

time: 233 us -> 95 us (0.41)
  waiting for transfers between devices: 107 us -> 0 us
  Pallas kernels: 0 us -> 89.8 us
  matrix products: 41 us -> 0 us
  blocking collectives: 32.6 us -> 0 us
  other arithmetic: 24.2 us -> 0 us
  between operations: 14.1 us -> 0.65 us
  local copies, waits for them, and re-layouts: 13.1 us -> 5.16 us
    psum x2 -> x0, waiting for transfers between devices: 107 us -> none  [the longest x1 55.3 us: draft_step(): down_sum = lax.psum(down_part, 'tp')]
    pallas_call x0 -> x3, Pallas kernels: none -> 89.8 us  [the longest x1 72.6 us: draft_step(): pl.pallas_call(functools.partial(main_kernel, n), out_shape=(pltpu.VMEM((...]
    dot_general x4 -> x0, matrix products: 41 us -> none  [the longest x1 30.3 us: draft_step(): logits = jnp.dot(out_norm, head_w, preferred_element_type=jnp.float32)]
    psum x1 -> x0, blocking collectives: 11.8 us -> none  [draft_step(): row_sum = lax.psum(jnp.sum(jnp.exp(shifted), axis=-1), 'tp')]
    pmax x1 -> x0, blocking collectives: 11.8 us -> none  [draft_step(): row_max = lax.pmax(jnp.max(logits, axis=-1), 'tp')]
    gather x1 -> x0, local copies, waits for them, and re-layouts: 11.6 us -> none  [draft_step(): jnp.take(embedding, jnp.clip(local_ids, 0, vocab_local - 1), axis=0)]
    reduce_sum x5 -> x0, other arithmetic: 9.7 us -> none  [the longest x1 5.57 us: draft_step(): row_sum = lax.psum(jnp.sum(jnp.exp(shifted), axis=-1), 'tp')]
    all_gather x1 -> x0, blocking collectives: 9.05 us -> none  [draft_step(): proj_full = lax.all_gather(proj_cols, 'tp', axis=1, tiled=True)]
  transfers between devices with their start and end apart: 2 -> 0, of which waited for: 2 -> 0; matrix products, arithmetic and copies ran while one was open for 1% -> 0% of each run, Pallas kernels for 0% -> 0%
where the time goes in v1:
time: 95 us; the launch traced here: 95.6 us
  Pallas kernels  89.8 us (95%)
  local copies, waits for them, and re-layouts  5.16 us (5%)
    pallas_call x1, Pallas kernels, draft_step(): pl.pallas_call(functools.partial(main_kernel, n), out_shape=(pltpu.VMEM((...  72.6 us
    pallas_call x1, Pallas kernels, draft_step(): pl.pallas_call(gather_kernel, out_shape=jax.ShapeDtypeStruct((rows, dim),...  11.5 us
    pallas_call x1, Pallas kernels, draft_step(): pl.pallas_call(close_kernel, grid=(pl.cdiv(vocab, depth),), out_shape=(ja...  5.66 us

profile of v1, /device:TPU:0, one launch (start us, length us, event | category | flops | bytes accessed | tf_op | source)
XLA Modules:
  0.0 95.6 jit_solution(15416558207778782241)
XLA Ops:
  0.6 1.3 %broadcast_in_dim.16.h_gain = f32[1,1536]{1,0:T(1,128)} reshape(f32[1536]{0:T(1024)} %param.16) | data formatting | bytes 12288 | tf_op jit(solution)/shard_map/broadcast_in_dim | solution.py:252
  1.9 1.3 %broadcast_in_dim.17.e_gain = f32[1,1536]{1,0:T(1,128)} reshape(f32[1536]{0:T(1024)} %param.17) | data formatting | bytes 12288 | tf_op jit(solution)/shard_map/broadcast_in_dim | solution.py:252
  3.2 1.3 %broadcast_in_dim.18.f_gain = f32[1,1536]{1,0:T(1,128)} reshape(f32[1536]{0:T(1024)} %param.18) | data formatting | bytes 12288 | tf_op jit(solution)/shard_map/broadcast_in_dim | solution.py:252
  4.5 1.3 %broadcast_in_dim.19.o_gain = f32[1,1536]{1,0:T(1,128)} reshape(f32[1536]{0:T(1024)} %param.19) | data formatting | bytes 12288 | tf_op jit(solution)/shard_map/broadcast_in_dim | solution.py:252
  5.8 11.5 %gather_rows.1.emb_ref = bf16[128,1536]{1,0:T(8,128)(2,1)} custom-call(s32[128]{0:T(128)} %ids_ref.1, s32[1,128]{1,0:T(1,128)} %bitcast.10, bf16[18992,1536]{1,0:T(8,128)(2,1)} %emb_ref.1), custom_call_target="tpu_custom_call" | custom-call | tf_op jit(solution)/shard_map/gather_rows/pallas_call | solution.py:222
  17.3 72.6 %draft_main.1 = (f32[18992,128]{1,0:T(8,128)S(1)}, f32[8,128]{1,0:T(8,128)S(1)}, bf16[1536,128]{1,0:T(8,128)(2,1)S(1)}) custom-call(bf16[128,1536]{1,0:T(8,128)(2,1)} %hidden_ref.1, bf16[128,1536]{1,0:T(8,128)(2,1)} %gather_rows.1.emb_ref, f32[1,1536]{1,0:T(1,128)} %broadcast_in_dim.16.h_gain, f32[1,1536]{1,0:T(1,128)} %broadcast_in_dim.17.e_gain, ...), custom_call_target="tpu_custom_call" | custom-call | tf_op jit(solution)/shard_map/draft_main/pallas_call | solution.py:232
  90.0 5.7 %close.1 = (f32[18992,128]{1,0:T(8,128)}, bf16[128,1536]{1,0:T(8,128)(2,1)}) custom-call(f32[18992,128]{1,0:T(8,128)S(1)} %get-tuple-element.7.z_ref, f32[8,128]{1,0:T(8,128)S(1)} %get-tuple-element.8.lse_ref, bf16[1536,128]{1,0:T(8,128)(2,1)S(1)} %get-tuple-element.9.u_in), custom_call_target="tpu_custom_call" | custom-call | tf_op jit(solution)/shard_map/close/pallas_call | solution.py:256

commit v2 on v1

v2 whole, which is shorter than its diff:
```python
import functools

import jax
import jax.numpy as jnp
from jax import lax
from jax.experimental import pallas as pl
from jax.experimental.pallas import tpu as pltpu
from jax.sharding import PartitionSpec as P

NORM_EPS = 1e-6
BLOCK = 1024
SLOTS = 12
MAIN_MIB = 17
PAIR = 3
HEAD_MIB = 17
CLOSE = 1024
MESH = pl.DeviceIdType.MESH
F32, BF16 = jnp.float32, jnp.bfloat16


def rms(values, gain, axis):
    wide = values.astype(F32)
    inv = lax.rsqrt(jnp.mean(wide * wide, axis=axis, keepdims=True) + NORM_EPS)
    return wide * inv * gain


def dot_t(a, b):
    return lax.dot_general(a, b, (((1,), (1,)), ((), ())), preferred_element_type=F32)


def gather_kernel(ids_ref, ids_row_ref, emb_ref, out_ref, buf, sem):
    rows, vocab = out_ref.shape[0], emb_ref.shape[0]
    base = lax.axis_index("tp") * vocab

    def issue(r, carry):
        local = jnp.clip(ids_ref[r] - base, 0, vocab - 1)
        start = pl.multiple_of((local // 8) * 8, 8)
        pltpu.make_async_copy(emb_ref.at[pl.ds(start, 8), :], buf.at[pl.ds(pl.multiple_of(r * 8, 8), 8), :], sem).start()
        return carry

    lax.fori_loop(0, rows, issue, 0, unroll=8)
    local = ids_row_ref[...] - base
    owned = (local >= 0) & (local < vocab)
    want = lax.broadcasted_iota(jnp.int32, (rows * 8, rows), 1) * 8 + (local & 7)
    here = lax.broadcasted_iota(jnp.int32, (rows * 8, rows), 0)
    pick = jnp.where((here == want) & owned, 1.0, 0.0).astype(BF16)
    pltpu.make_async_copy(emb_ref.at[pl.ds(0, rows * 8), :], buf, sem).wait()
    out_ref[...] = lax.dot_general(pick, buf[...], (((0,), (0,)), ((), ())), preferred_element_type=F32).astype(BF16)


def main_kernel(n, hidden_ref, emb_ref, h_gain, e_gain, f_gain, o_gain,
                proj_hbm, gate_hbm, up_hbm, down_hbm, head_hbm,
                ring, o_v, o_rows, u_ref,
                proj_v, gate_v, up_v, down_v, emb_pair, emb_sum, emb_in, emb_mine, emb_all, p_mine, p_all,
                part_v, pair_in, sum_v, part_in, u_mine, u_all, f_wide, o_wide,
                w_sem, ring_sem, send_sem, recv_sem):
    me = lax.axis_index("tp")
    rows, dim = hidden_ref.shape
    chunk, half = rows // n, rows // 2
    cols = p_mine.shape[0]

    core, chip = lax.rem(me, 2), lax.div(me, 2)
    partner = me + 1 - 2 * core
    x, y = lax.rem(chip, 2), lax.div(chip, 2)
    chips = (chip, chip + 1 - 2 * x, chip + 2 - 4 * y, 3 - chip)
    far = (3, 1, 2)

    weights = [pltpu.make_async_copy(src, dst, w_sem.at[i]) for i, (src, dst) in enumerate(
        ((proj_hbm, proj_v), (gate_hbm, gate_v), (up_hbm, up_v), (down_hbm, down_v)))]
    for copy in weights:
        copy.start()

    def head_copy(t):
        at = pl.ds(pl.multiple_of(t * BLOCK, BLOCK), BLOCK)
        return pltpu.make_async_copy(head_hbm.at[at, :], ring.at[at, :], ring_sem.at[t])

    barrier = pltpu.get_barrier_semaphore()
    for d in range(1, n):
        pl.semaphore_signal(barrier, inc=1, device_id={"tp": lax.rem(me + d, n)}, device_id_type=MESH)
    normed_h = rms(hidden_ref[...], h_gain[...][None, :], -1).astype(BF16)
    pl.semaphore_wait(barrier, n - 1)

    sent = []

    def send(source, target, device):
        i = len(sent)
        copy = pltpu.make_async_remote_copy(src_ref=source, dst_ref=target, send_sem=send_sem.at[i], recv_sem=recv_sem.at[i],
                                            device_id={"tp": device}, device_id_type=MESH)
        copy.start()
        sent.append(copy)
        return copy

    def part(ref, j, size):
        return ref.at[pl.ds(pl.multiple_of(j * size, size), size), :]

    def all_gather(mine, place):
        arriving = {m: send(mine, place(me), chips[m] * 2 + core) for m in far}
        beside = [send(mine, place(me), partner)]
        place(me)[...] = mine[...]
        for m in (1, 2, 3):
            arriving[m].wait_recv()
            there = place(chips[m] * 2 + core)
            beside.append(send(there, there, partner))
        for copy in beside:
            copy.wait_recv()

    pair = send(part(emb_ref, 1 - core, half), emb_pair, partner)

    def prefetch(t, carry):
        head_copy(t).start()
        return carry

    lax.fori_loop(0, SLOTS, prefetch, 0)
    pair.wait_recv()
    emb_sum[...] = part(emb_ref, core, half)[...] + emb_pair[...]
    first = [send(part(emb_sum, chips[m], chunk), emb_in.at[m - 1], chips[m] * 2 + core) for m in far]
    weights[0].wait()
    acc_h = dot_t(proj_v[:, :dim], normed_h)
    total = part(emb_sum, chip, chunk)[...].astype(F32)
    for copy in first:
        copy.wait_recv()
    for m in (0, 1, 2):
        total = total + emb_in[m].astype(F32)
    emb_mine[...] = rms(total, e_gain[...][None, :], -1).astype(BF16)
    all_gather(emb_mine, lambda j: part(emb_all, lax.rem(j, 2) * (n // 2) + lax.div(j, 2), chunk))
    p_mine[...] = (acc_h + dot_t(proj_v[:, dim:], emb_all[...])).astype(BF16)

    all_gather(p_mine, lambda j: part(p_all, j, cols))
    f_wide[...] = jnp.transpose(jnp.broadcast_to(f_gain[...][None, :], (rows, dim)))
    normed = rms(p_all[...], f_wide[...], 0).astype(BF16)
    weights[1].wait()
    gate = jnp.dot(gate_v[...], normed, preferred_element_type=F32)
    weights[2].wait()
    up = jnp.dot(up_v[...], normed, preferred_element_type=F32)
    act = jnp.transpose((jax.nn.silu(gate) * up).astype(BF16))
    weights[3].wait()

    pairs = {}
    for m in (3, 1, 2, 0):
        block = jnp.dot(act, down_v[:, pl.ds(pl.multiple_of(chips[m] * 2 * cols, 2 * cols), 2 * cols)], preferred_element_type=F32)
        part_v[m] = jnp.transpose(block)
        pairs[m] = send(part_v.at[m, pl.ds(pl.multiple_of((1 - core) * cols, cols), cols), :], pair_in.at[m], partner)
    mine = pl.ds(pl.multiple_of(core * cols, cols), cols)
    arriving = []
    for m in far:
        pairs[m].wait_recv()
        sum_v[m - 1] = part_v[m, mine, :] + pair_in[m]
        arriving.append(send(sum_v.at[m - 1], part_in.at[m - 1], chips[m] * 2 + core))
    pairs[0].wait_recv()
    total = part_v[0, mine, :] + pair_in[0]
    for copy in arriving:
        copy.wait_recv()
    for m in (0, 1, 2):
        total = total + part_in[m]
    u_mine[...] = (p_mine[...].astype(F32) + total).astype(BF16)
    o_wide[...] = jnp.transpose(jnp.broadcast_to(o_gain[...][None, :], (rows, dim)))
    all_gather(u_mine, lambda j: part(u_all, j, cols))
    normed_o = rms(u_all[...], o_wide[...], 0).astype(BF16)
    o_v[:, :rows] = normed_o
    o_v[:, rows:] = jnp.zeros_like(normed_o)
    o_rows[...] = jnp.transpose(normed_o)
    u_ref[...] = u_all[...]

    def drain(t, carry):
        head_copy(t).wait()
        return carry

    lax.fori_loop(0, SLOTS, drain, 0)
    for copy in sent:
        copy.wait_send()


def head_kernel(ring, o_v, o_rows, head_hbm, z_ref, stat_ref, stream, end_v, m_v, s_v, stream_sem):
    rows, dim = o_rows.shape
    vocab = head_hbm.shape[0]
    blocks = vocab // BLOCK
    rest = vocab - blocks * BLOCK
    pair = stream.shape[0]
    trips = (blocks - SLOTS) // pair
    held = SLOTS // trips

    def stream_copy(t, b):
        at = pl.multiple_of((SLOTS + t * pair + b) * BLOCK, BLOCK)
        return pltpu.make_async_copy(head_hbm.at[pl.ds(at, BLOCK), :], stream.at[b], stream_sem.at[b])

    end_copy = pltpu.make_async_copy(head_hbm.at[pl.ds(blocks * BLOCK, rest), :], end_v, stream_sem.at[pair])
    for b in range(pair):
        stream_copy(0, b).start()
    end_copy.start()

    m_v[...] = jnp.full_like(m_v, -jnp.inf)
    s_v[...] = jnp.zeros_like(s_v)

    def fold(block):
        groups = block.reshape(block.shape[0] // 8, 8, rows)
        old = m_v[...]
        new = jnp.maximum(old, jnp.max(groups, axis=0))
        s_v[...] = s_v[...] * jnp.exp(old - new) + jnp.sum(jnp.exp(groups - new[None]), axis=0)
        m_v[...] = new

    def head(*accs):
        def trip(i, carry):
            steps = [(b, k) for b in range(held + pair) for k in range(dim // 256)]

            def weights(b, at, k):
                lanes = slice(k * 256, (k + 1) * 256)
                if b < held:
                    return ring[pl.ds(pl.multiple_of((i * held + b) * BLOCK + at, 256), 256), lanes]
                return stream[b - held, at:at + 256, lanes]

            def push_w(j):
                b, k = steps[j]
                if b >= held and k == 0:
                    stream_copy(i, b - held).wait()
                for q in (0, 1):
                    pltpu.matmul_push_rhs(weights(b, q * 512, k), staging_register=0, mxu_index=q, transpose=True)

            def push_o(j):
                k = steps[j][1]
                for q in (0, 1):
                    pltpu.matmul_push_rhs(o_v[k * 256:(k + 1) * 256, :], staging_register=1, mxu_index=q, transpose=False)

            def pops(b):
                block = i * held + b if b < held else SLOTS + i * pair + b - held
                at = pl.multiple_of(block * BLOCK, BLOCK)
                for q in (0, 1):
                    block = jnp.transpose(pltpu.matmul_pop(accs[q * 4 + b % 2 * 2]))
                    z_ref[pl.ds(at + q * 512, 256), :] = block
                    fold(block)
                    block = pltpu.matmul_pop(accs[q * 4 + b % 2 * 2 + 1])[:, :rows]
                    z_ref[pl.ds(at + q * 512 + 256, 256), :] = block
                    fold(block)

            push_w(0)
            push_o(0)
            for j, (b, k) in enumerate(steps):
                for q in (0, 1):
                    pltpu.matmul_acc_lhs(accs[q * 4 + b % 2 * 2], o_rows[:, k * 256:(k + 1) * 256], load_staged_rhs=0)
                if j + 1 < len(steps):
                    push_w(j + 1)
                for q in (0, 1):
                    pltpu.matmul_acc_lhs(accs[q * 4 + b % 2 * 2 + 1], weights(b, q * 512 + 256, k), load_staged_rhs=1)
                if j + 1 < len(steps):
                    push_o(j + 1)
                if k == 2 and b > 0:
                    pops(b - 1)
            pops(held + pair - 1)

            @pl.when(i + 1 < trips)
            def _():
                for b in range(pair):
                    stream_copy(i + 1, b).start()
            return carry

        lax.fori_loop(0, trips, trip, 0)

    pl.run_scoped(head, *[pltpu.ACC(q)((size, 256), F32) for q in (0, 1) for _ in (0, 1) for size in (128, 256)])
    end_copy.wait()
    first_rows = rest // 32 * 16
    sizes = (first_rows, rest - first_rows)

    def tail(*accs):
        for k in range(dim // 256):
            for q in (0, 1):
                pltpu.matmul_push_rhs(o_v[k * 256:(k + 1) * 256, :], staging_register=k % 2, mxu_index=q, transpose=False)
                pltpu.matmul_acc_lhs(accs[q], end_v[q * sizes[0]:q * sizes[0] + sizes[q], k * 256:(k + 1) * 256], load_staged_rhs=k % 2)
        for q in (0, 1):
            block = pltpu.matmul_pop(accs[q])[:, :rows]
            z_ref[pl.ds(blocks * BLOCK + q * sizes[0], sizes[q]), :] = block
            fold(block)

    pl.run_scoped(tail, *[pltpu.ACC(q)((sizes[q], 256), F32) for q in (0, 1)])
    m_row = jnp.max(m_v[...], axis=0, keepdims=True)
    s_row = jnp.sum(s_v[...] * jnp.exp(m_v[...] - m_row), axis=0, keepdims=True)
    stat_ref[...] = jnp.concatenate([m_row, s_row, jnp.zeros((6, rows), F32)], axis=0)


def total_kernel(n, stat_ref, lse_ref, stat_in, send_sem, recv_sem):
    me = lax.axis_index("tp")
    barrier = pltpu.get_barrier_semaphore()
    for d in range(1, n):
        pl.semaphore_signal(barrier, inc=1, device_id={"tp": lax.rem(me + d, n)}, device_id_type=MESH)
    stat_in[me] = stat_ref[...]
    pl.semaphore_wait(barrier, n - 1)
    copies = []
    for d in (4, 6, 2, 3, 5, 7, 1):
        copies.append(pltpu.make_async_remote_copy(
            src_ref=stat_ref, dst_ref=stat_in.at[me], send_sem=send_sem.at[d - 1], recv_sem=recv_sem.at[d - 1],
            device_id={"tp": lax.rem(me + d, n)}, device_id_type=MESH))
        copies[-1].start()
    for copy in copies:
        copy.wait_recv()
    stats = stat_in[...]
    m_all, s_all = stats[:, 0, :], stats[:, 1, :]
    m_top = jnp.max(m_all, axis=0, keepdims=True)
    lse = m_top + jnp.log(jnp.sum(s_all * jnp.exp(m_all - m_top), axis=0, keepdims=True))
    lse_ref[...] = jnp.broadcast_to(lse, lse_ref.shape)
    for copy in copies:
        copy.wait_send()


def close_kernel(z_ref, lse_ref, u_in, logp_hbm, u_hbm, stage, u_stage, sem):
    vocab = z_ref.shape[0]
    copies = []
    for i, at in enumerate(range(0, vocab, CLOSE)):
        size = min(CLOSE, vocab - at)
        stage[at:at + size, :] = z_ref[at:at + size, :] - lse_ref[0:1, :]
        copies.append(pltpu.make_async_copy(stage.at[pl.ds(at, size), :], logp_hbm.at[pl.ds(at, size), :], sem.at[i]))
        copies[-1].start()
    u_stage[...] = jnp.transpose(u_in[...])
    copies.append(pltpu.make_async_copy(u_stage, u_hbm, sem.at[len(copies)]))
    copies[-1].start()
    for copy in copies:
        copy.wait()


def solution(mesh):
    n = mesh.shape["tp"]

    def draft_step(hidden, tokens, embedding, head_w, h_norm, e_norm, f_norm, o_norm, proj_w, w_gate, w_up, w_down):
        rows, dim = hidden.shape
        vocab = head_w.shape[1]
        cols, ffn = proj_w.shape[1], w_gate.shape[1]
        chunk = rows // n
        smem = pl.BlockSpec(memory_space=pltpu.SMEM)
        vmem = pl.BlockSpec(memory_space=pltpu.VMEM)
        hbm = pl.BlockSpec(memory_space=pl.ANY)
        emb_rows = pl.pallas_call(
            gather_kernel,
            out_shape=jax.ShapeDtypeStruct((rows, dim), BF16),
            in_specs=[smem, vmem, hbm],
            out_specs=vmem,
            scratch_shapes=[pltpu.VMEM((rows * 8, dim), BF16), pltpu.SemaphoreType.DMA],
            name="gather_rows",
        )(tokens, tokens[None, :], embedding)

        dma = pltpu.SemaphoreType.DMA
        head_t = head_w.T
        ring, o_pad, o_rows, u = pl.pallas_call(
            functools.partial(main_kernel, n),
            out_shape=(pltpu.VMEM((SLOTS * BLOCK, dim), BF16), pltpu.VMEM((dim, 2 * rows), BF16), pltpu.VMEM((rows, dim), BF16),
                       pltpu.VMEM((dim, rows), BF16)),
            in_specs=[vmem] * 6 + [hbm] * 5,
            out_specs=(vmem, vmem, vmem, vmem),
            scratch_shapes=[
                pltpu.VMEM((cols, 2 * dim), BF16), pltpu.VMEM((ffn, dim), BF16), pltpu.VMEM((ffn, dim), BF16),
                pltpu.VMEM((ffn, dim), BF16),
                pltpu.VMEM((rows // 2, dim), BF16), pltpu.VMEM((rows // 2, dim), BF16), pltpu.VMEM((3, chunk, dim), BF16),
                pltpu.VMEM((chunk, dim), BF16), pltpu.VMEM((rows, dim), BF16),
                pltpu.VMEM((cols, rows), BF16), pltpu.VMEM((dim, rows), BF16),
                pltpu.VMEM((4, 2 * cols, rows), F32), pltpu.VMEM((4, cols, rows), F32), pltpu.VMEM((3, cols, rows), F32),
                pltpu.VMEM((3, cols, rows), F32),
                pltpu.VMEM((cols, rows), BF16), pltpu.VMEM((dim, rows), BF16),
                pltpu.VMEM((dim, rows), F32), pltpu.VMEM((dim, rows), F32),
                dma((4,)), dma((SLOTS,)), dma((40,)), dma((40,)),
            ],
            compiler_params=pltpu.CompilerParams(
                collective_id=0, has_side_effects=True, vmem_limit_bytes=int(MAIN_MIB * 1024 * 1024)),
            name="draft_main",
        )(hidden, emb_rows, h_norm, e_norm, f_norm, o_norm,
          proj_w.T, w_gate.T, w_up.T, w_down, head_t)

        z, stat = pl.pallas_call(
            head_kernel,
            out_shape=(pltpu.VMEM((vocab, rows), F32), pltpu.VMEM((8, rows), F32)),
            in_specs=[vmem, vmem, vmem, hbm],
            out_specs=(vmem, vmem),
            scratch_shapes=[
                pltpu.VMEM((PAIR, BLOCK, dim), BF16), pltpu.VMEM((vocab % BLOCK, dim), BF16),
                pltpu.VMEM((8, rows), F32), pltpu.VMEM((8, rows), F32), dma((PAIR + 1,))],
            compiler_params=pltpu.CompilerParams(vmem_limit_bytes=int(HEAD_MIB * 1024 * 1024)),
            name="head",
        )(*(pltpu.with_memory_space_constraint(v, pltpu.VMEM) for v in (ring, o_pad, o_rows)), head_t)

        lse = pl.pallas_call(
            functools.partial(total_kernel, n),
            out_shape=pltpu.VMEM((8, rows), F32),
            in_specs=[vmem],
            out_specs=vmem,
            scratch_shapes=[pltpu.VMEM((n, 8, rows), F32), dma((n - 1,)), dma((n - 1,))],
            compiler_params=pltpu.CompilerParams(collective_id=1, has_side_effects=True, vmem_limit_bytes=4 * 1024 * 1024),
            name="total",
        )(stat)

        logp, new_u = pl.pallas_call(
            close_kernel,
            out_shape=(jax.ShapeDtypeStruct((vocab, rows), F32), jax.ShapeDtypeStruct((rows, dim), BF16)),
            in_specs=[vmem, vmem, vmem],
            out_specs=(hbm, hbm),
            scratch_shapes=[pltpu.VMEM((vocab, rows), F32), pltpu.VMEM((rows, dim), BF16), dma((pl.cdiv(vocab, CLOSE) + 1,))],
            compiler_params=pltpu.CompilerParams(vmem_limit_bytes=16 * 1024 * 1024),
            name="close",
        )(z, lse, u)
        return new_u, logp.T

    specs_in = (P("dp", None), P("dp"), P("tp", None), P(None, "tp"), P(None), P(None), P(None), P(None), P(None, "tp"), P(None, "tp"), P(None, "tp"), P("tp", None))
    specs_out = (P("dp", None), P("dp", "tp"))
    return jax.shard_map(draft_step, mesh=mesh, in_specs=specs_in, out_specs=specs_out, check_vma=False)
```

time: 95 us -> 72.3 us (0.76); the launches traced: 95.6 us -> 71.4 us
  Pallas kernels: 89.8 us -> 70.8 us
  local copies, waits for them, and re-layouts: 5.16 us -> 0 us
    pallas_call x1, Pallas kernels: 72.6 us -> 37.2 us  [draft_step(): pl.pallas_call(functools.partial(main_kernel, n), out_shape=(pltpu.VMEM((...]
    pallas_call x1 -> x3, Pallas kernels: 5.66 us -> 22.1 us  [the longest x1 12.7 us: draft_step(): pl.pallas_call(head_kernel, out_shape=(pltpu.VMEM((vocab, rows), F32), pl...]
    broadcast_in_dim x4 -> x0, local copies, waits for them, and re-layouts: 5.16 us -> none  [the longest x1 1.29 us: draft_step(): h_norm[None]]
where the time goes in v2:
time: 72.3 us; the launch traced here: 71.4 us
  Pallas kernels  70.8 us (98%)
    pallas_call x1, Pallas kernels, draft_step(): pl.pallas_call(functools.partial(main_kernel, n), out_shape=(pltpu.VMEM((...  37.2 us
    pallas_call x1, Pallas kernels, draft_step(): pl.pallas_call(head_kernel, out_shape=(pltpu.VMEM((vocab, rows), F32), pl...  12.7 us
    pallas_call x1, Pallas kernels, draft_step(): pl.pallas_call(gather_kernel, out_shape=jax.ShapeDtypeStruct((rows, dim),...  11.4 us
    pallas_call x1, Pallas kernels, draft_step(): pl.pallas_call(functools.partial(total_kernel, n), out_shape=pltpu.VMEM((...  5.31 us
    pallas_call x1, Pallas kernels, draft_step(): pl.pallas_call(close_kernel, out_shape=(jax.ShapeDtypeStruct((vocab, rows...  4.09 us

profile of v2, /device:TPU:0, one launch (start us, length us, event | category | flops | bytes accessed | tf_op | source)
XLA Modules:
  0.0 71.4 jit_solution(7939225576942307979)
XLA Ops:
  0.6 11.4 %gather_rows.1.emb_ref = bf16[128,1536]{1,0:T(8,128)(2,1)} custom-call(s32[128]{0:T(128)} %ids_ref.1, s32[1,128]{1,0:T(1,128)} %bitcast.11, bf16[18992,1536]{1,0:T(8,128)(2,1)} %emb_ref.1), custom_call_target="tpu_custom_call" | custom-call | tf_op jit(solution)/shard_map/gather_rows/pallas_call | solution.py:328
  12.1 37.2 %draft_main.1 = (bf16[12288,1536]{1,0:T(8,128)(2,1)S(1)}, bf16[1536,256]{1,0:T(8,128)(2,1)S(1)}, bf16[128,1536]{1,0:T(8,128)(2,1)S(1)}, bf16[1536,128]{1,0:T(8,128)(2,1)S(1)}) custom-call(bf16[128,1536]{1,0:T(8,128)(2,1)} %hidden_ref.1, bf16[128,1536]{1,0:T(8,128)(2,1)} %gather_rows.1.emb_ref, f32[1536]{0:T(1024)} %h_gain.1, f32[1536]{0:T(1024)} %e_gain.1, ...), custom_call_target="tpu_custom_call" | custom-call | tf_op jit(solution)/shard_map/draft_main/pallas_call | solution.py:339
  49.3 12.7 %head.1 = (f32[18992,128]{1,0:T(8,128)S(1)}, f32[8,128]{1,0:T(8,128)S(1)}) custom-call(bf16[12288,1536]{1,0:T(8,128)(2,1)S(1)} %get-tuple-element.10.ring, bf16[1536,256]{1,0:T(8,128)(2,1)S(1)} %get-tuple-element.11.o_v, bf16[128,1536]{1,0:T(8,128)(2,1)S(1)} %get-tuple-element.12.o_rows, bf16[18992,1536]{1,0:T(8,128)(2,1)} %bitcast.7), custom_call_target="tpu_custom_call" | custom-call | tf_op jit(solution)/shard_map/head/pallas_call | solution.py:363
  62.0 5.3 %total.1.lse_ref = f32[8,128]{1,0:T(8,128)S(1)} custom-call(f32[8,128]{1,0:T(8,128)S(1)} %get-tuple-element.14.stat_ref), custom_call_target="tpu_custom_call" | custom-call | tf_op jit(solution)/shard_map/total/pallas_call | solution.py:375
  67.3 4.1 %close.1 = (f32[18992,128]{1,0:T(8,128)}, bf16[128,1536]{1,0:T(8,128)(2,1)}) custom-call(f32[18992,128]{1,0:T(8,128)S(1)} %get-tuple-element.13.z_ref, f32[8,128]{1,0:T(8,128)S(1)} %total.1.lse_ref, bf16[1536,128]{1,0:T(8,128)(2,1)S(1)} %get-tuple-element.15.u_in), custom_call_target="tpu_custom_call" | custom-call | tf_op jit(solution)/shard_map/close/pallas_call | solution.py:385

commit v3 on v2

--- a/solution.py
+++ b/solution.py
@@ -9,10 +9,11 @@
 
 NORM_EPS = 1e-6
 BLOCK = 1024
-SLOTS = 12
-MAIN_MIB = 17
-PAIR = 3
-HEAD_MIB = 17
+SLOTS = 10
+MAIN_MIB = 23.4
+PAIR = 4
+HEAD_MIB = 23.4
+GATHER_MIB = 60
 CLOSE = 1024
 MESH = pl.DeviceIdType.MESH
 F32, BF16 = jnp.float32, jnp.bfloat16
@@ -28,36 +29,43 @@
     return lax.dot_general(a, b, (((1,), (1,)), ((), ())), preferred_element_type=F32)
 
 
-def gather_kernel(ids_ref, ids_row_ref, emb_ref, out_ref, buf, sem):
-    rows, vocab = out_ref.shape[0], emb_ref.shape[0]
+def gather_kernel(ids_ref, ids_row_ref, emb_hbm, hidden_hbm, h_gain, e_gain, emb_ref, hid_ref, buf, hid_v, sem):
+    rows, dim = emb_ref.shape
+    vocab = emb_hbm.shape[0]
     base = lax.axis_index("tp") * vocab
 
     def issue(r, carry):
-        local = jnp.clip(ids_ref[r] - base, 0, vocab - 1)
+        local = ids_ref[r] - base
+        local = jnp.where((local >= 0) & (local < vocab), local, r * 8)
         start = pl.multiple_of((local // 8) * 8, 8)
-        pltpu.make_async_copy(emb_ref.at[pl.ds(start, 8), :], buf.at[pl.ds(pl.multiple_of(r * 8, 8), 8), :], sem).start()
+        pltpu.make_async_copy(emb_hbm.at[pl.ds(start, 8), :], buf.at[pl.ds(pl.multiple_of(r * 8, 8), 8), :], sem.at[0]).start()
         return carry
 
-    lax.fori_loop(0, rows, issue, 0, unroll=8)
+    lax.fori_loop(0, rows, issue, 0, unroll=16)
+    hid_copy = pltpu.make_async_copy(hidden_hbm, hid_v, sem.at[1])
+    hid_copy.start()
     local = ids_row_ref[...] - base
     owned = (local >= 0) & (local < vocab)
     want = lax.broadcasted_iota(jnp.int32, (rows * 8, rows), 1) * 8 + (local & 7)
     here = lax.broadcasted_iota(jnp.int32, (rows * 8, rows), 0)
     pick = jnp.where((here == want) & owned, 1.0, 0.0).astype(BF16)
-    pltpu.make_async_copy(emb_ref.at[pl.ds(0, rows * 8), :], buf, sem).wait()
-    out_ref[...] = lax.dot_general(pick, buf[...], (((0,), (0,)), ((), ())), preferred_element_type=F32).astype(BF16)
-
-
-def main_kernel(n, hidden_ref, emb_ref, h_gain, e_gain, f_gain, o_gain,
+    hid_copy.wait()
+    hid_ref[...] = rms(hid_v[...], h_gain[...][None, :], -1).astype(BF16)
+    pltpu.make_async_copy(emb_hbm.at[pl.ds(0, rows * 8), :], buf, sem.at[0]).wait()
+    picked = lax.dot_general(pick, buf[...], (((0,), (0,)), ((), ())), preferred_element_type=F32)
+    emb_ref[...] = rms(picked, e_gain[...][None, :], -1).astype(BF16)
+
+
+def main_kernel(n, emb_hbm, hid_hbm, f_gain, o_gain,
                 proj_hbm, gate_hbm, up_hbm, down_hbm, head_hbm,
                 ring, o_v, o_rows, u_ref,
-                proj_v, gate_v, up_v, down_v, emb_pair, emb_sum, emb_in, emb_mine, emb_all, p_mine, p_all,
-                part_v, pair_in, sum_v, part_in, u_mine, u_all, f_wide, o_wide,
+                emb_ref, hid_ref, proj_v, gate_v, up_v, wide_w, down_v, emb_pair, emb_in, emb_mine, emb_all, p_mine, p_all,
+                part_v, pair_in, part_in, u_mine, u_all, wide,
                 w_sem, ring_sem, send_sem, recv_sem):
     me = lax.axis_index("tp")
-    rows, dim = hidden_ref.shape
+    rows, dim = hid_ref.shape
     chunk, half = rows // n, rows // 2
-    cols = p_mine.shape[0]
+    cols, ffn = p_mine.shape[0], gate_hbm.shape[0]
 
     core, chip = lax.rem(me, 2), lax.div(me, 2)
     partner = me + 1 - 2 * core
@@ -65,6 +73,9 @@
     chips = (chip, chip + 1 - 2 * x, chip + 2 - 4 * y, 3 - chip)
     far = (3, 1, 2)
 
+    local = [pltpu.make_async_copy(src, dst, w_sem.at[4 + i]) for i, (src, dst) in enumerate(((emb_hbm, emb_ref), (hid_hbm, hid_ref)))]
+    for copy in local:
+        copy.start()
     weights = [pltpu.make_async_copy(src, dst, w_sem.at[i]) for i, (src, dst) in enumerate(
         ((proj_hbm, proj_v), (gate_hbm, gate_v), (up_hbm, up_v), (down_hbm, down_v)))]
     for copy in weights:
@@ -77,7 +88,7 @@
     barrier = pltpu.get_barrier_semaphore()
     for d in range(1, n):
         pl.semaphore_signal(barrier, inc=1, device_id={"tp": lax.rem(me + d, n)}, device_id_type=MESH)
-    normed_h = rms(hidden_ref[...], h_gain[...][None, :], -1).astype(BF16)
+    local[0].wait()
     pl.semaphore_wait(barrier, n - 1)
 
     sent = []
@@ -93,10 +104,11 @@
     def part(ref, j, size):
         return ref.at[pl.ds(pl.multiple_of(j * size, size), size), :]
 
-    def all_gather(mine, place):
+    def all_gather(mine, place, meanwhile=lambda: None):
         arriving = {m: send(mine, place(me), chips[m] * 2 + core) for m in far}
         beside = [send(mine, place(me), partner)]
         place(me)[...] = mine[...]
+        meanwhile()
         for m in (1, 2, 3):
             arriving[m].wait_recv()
             there = place(chips[m] * 2 + core)
@@ -112,27 +124,36 @@
 
     lax.fori_loop(0, SLOTS, prefetch, 0)
     pair.wait_recv()
-    emb_sum[...] = part(emb_ref, core, half)[...] + emb_pair[...]
-    first = [send(part(emb_sum, chips[m], chunk), emb_in.at[m - 1], chips[m] * 2 + core) for m in far]
+    emb_sum = part(emb_ref, core, half)
+    emb_sum[...] = emb_sum[...] + emb_pair[...]
+    first = [send(part(emb_ref, core * (n // 2) + chips[m], chunk), emb_in.at[m - 1], chips[m] * 2 + core) for m in far]
+    turned = pl.cdiv(ffn, 128) * 128
+
+    def turn(i):
+        weights[1 + i].wait()
+        source = (gate_v, up_v)[i]
+        for at in range(0, ffn, 256):
+            size = min(256, ffn - at)
+            wide_w[:, i * turned + at:i * turned + at + size] = jnp.transpose(source[at:at + size, :])
+
     weights[0].wait()
-    acc_h = dot_t(proj_v[:, :dim], normed_h)
-    total = part(emb_sum, chip, chunk)[...].astype(F32)
+    local[1].wait()
+    acc_h = dot_t(proj_v[:, :dim], hid_ref[...])
+    wide[...] = jnp.transpose(jnp.broadcast_to(f_gain[...][None, :], (rows, dim)))
+    turn(0)
+    total = part(emb_ref, core * (n // 2) + chip, chunk)[...]
     for copy in first:
         copy.wait_recv()
     for m in (0, 1, 2):
-        total = total + emb_in[m].astype(F32)
-    emb_mine[...] = rms(total, e_gain[...][None, :], -1).astype(BF16)
-    all_gather(emb_mine, lambda j: part(emb_all, lax.rem(j, 2) * (n // 2) + lax.div(j, 2), chunk))
+        total = total + emb_in[m]
+    emb_mine[...] = total
+    all_gather(emb_mine, lambda j: part(emb_all, lax.rem(j, 2) * (n // 2) + lax.div(j, 2), chunk), lambda: turn(1))
     p_mine[...] = (acc_h + dot_t(proj_v[:, dim:], emb_all[...])).astype(BF16)
 
     all_gather(p_mine, lambda j: part(p_all, j, cols))
-    f_wide[...] = jnp.transpose(jnp.broadcast_to(f_gain[...][None, :], (rows, dim)))
-    normed = rms(p_all[...], f_wide[...], 0).astype(BF16)
-    weights[1].wait()
-    gate = jnp.dot(gate_v[...], normed, preferred_element_type=F32)
-    weights[2].wait()
-    up = jnp.dot(up_v[...], normed, preferred_element_type=F32)
-    act = jnp.transpose((jax.nn.silu(gate) * up).astype(BF16))
+    normed = rms(p_all[...], wide[...], 0).astype(BF16)
+    hidden = jnp.dot(jnp.transpose(normed), wide_w[...], preferred_element_type=F32)
+    act = (jax.nn.silu(hidden[:, :ffn]) * hidden[:, turned:turned + ffn]).astype(BF16)
     weights[3].wait()
 
     pairs = {}
@@ -144,20 +165,19 @@
     arriving = []
     for m in far:
         pairs[m].wait_recv()
-        sum_v[m - 1] = part_v[m, mine, :] + pair_in[m]
-        arriving.append(send(sum_v.at[m - 1], part_in.at[m - 1], chips[m] * 2 + core))
+        part_v[m, mine, :] = part_v[m, mine, :] + pair_in[m]
+        arriving.append(send(part_v.at[m, mine, :], part_in.at[m - 1], chips[m] * 2 + core))
     pairs[0].wait_recv()
     total = part_v[0, mine, :] + pair_in[0]
+    wide[...] = jnp.transpose(jnp.broadcast_to(o_gain[...][None, :], (rows, dim)))
     for copy in arriving:
         copy.wait_recv()
     for m in (0, 1, 2):
         total = total + part_in[m]
     u_mine[...] = (p_mine[...].astype(F32) + total).astype(BF16)
-    o_wide[...] = jnp.transpose(jnp.broadcast_to(o_gain[...][None, :], (rows, dim)))
     all_gather(u_mine, lambda j: part(u_all, j, cols))
-    normed_o = rms(u_all[...], o_wide[...], 0).astype(BF16)
-    o_v[:, :rows] = normed_o
-    o_v[:, rows:] = jnp.zeros_like(normed_o)
+    normed_o = rms(u_all[...], wide[...], 0).astype(BF16)
+    o_v[...] = normed_o
     o_rows[...] = jnp.transpose(normed_o)
     u_ref[...] = u_all[...]
 
@@ -170,7 +190,7 @@
         copy.wait_send()
 
 
-def head_kernel(ring, o_v, o_rows, head_hbm, z_ref, stat_ref, stream, end_v, m_v, s_v, stream_sem):
+def head_kernel(ring, o_in, o_rows, head_hbm, z_ref, stat_ref, stream, end_v, o_v, m_v, s_v, stream_sem):
     rows, dim = o_rows.shape
     vocab = head_hbm.shape[0]
     blocks = vocab // BLOCK
@@ -187,6 +207,8 @@
     for b in range(pair):
         stream_copy(0, b).start()
     end_copy.start()
+    o_v[:, :rows] = o_in[...]
+    o_v[:, rows:] = jnp.zeros_like(o_in[...])
 
     m_v[...] = jnp.full_like(m_v, -jnp.inf)
     s_v[...] = jnp.zeros_like(s_v)
@@ -325,40 +347,42 @@
         smem = pl.BlockSpec(memory_space=pltpu.SMEM)
         vmem = pl.BlockSpec(memory_space=pltpu.VMEM)
         hbm = pl.BlockSpec(memory_space=pl.ANY)
-        emb_rows = pl.pallas_call(
+        dma = pltpu.SemaphoreType.DMA
+        on_chip = functools.partial(pltpu.with_memory_space_constraint, memory_space=pltpu.VMEM)
+        ready = pl.pallas_call(
             gather_kernel,
-            out_shape=jax.ShapeDtypeStruct((rows, dim), BF16),
-            in_specs=[smem, vmem, hbm],
-            out_specs=vmem,
-            scratch_shapes=[pltpu.VMEM((rows * 8, dim), BF16), pltpu.SemaphoreType.DMA],
+            out_shape=(jax.ShapeDtypeStruct((rows, dim), BF16),) * 2,
+            in_specs=[smem, vmem, hbm, hbm, vmem, vmem],
+            out_specs=(vmem, vmem),
+            scratch_shapes=[pltpu.VMEM((rows * 8, dim), BF16), pltpu.VMEM((rows, dim), BF16), dma((2,))],
+            compiler_params=pltpu.CompilerParams(vmem_limit_bytes=GATHER_MIB * 1024 * 1024),
             name="gather_rows",
-        )(tokens, tokens[None, :], embedding)
-
-        dma = pltpu.SemaphoreType.DMA
+        )(tokens, tokens[None, :], embedding, hidden, h_norm, e_norm)
+
         head_t = head_w.T
-        ring, o_pad, o_rows, u = pl.pallas_call(
+        ring, o_cols, o_rows, u = pl.pallas_call(
             functools.partial(main_kernel, n),
-            out_shape=(pltpu.VMEM((SLOTS * BLOCK, dim), BF16), pltpu.VMEM((dim, 2 * rows), BF16), pltpu.VMEM((rows, dim), BF16),
+            out_shape=(pltpu.VMEM((SLOTS * BLOCK, dim), BF16), pltpu.VMEM((dim, rows), BF16), pltpu.VMEM((rows, dim), BF16),
                        pltpu.VMEM((dim, rows), BF16)),
-            in_specs=[vmem] * 6 + [hbm] * 5,
+            in_specs=[hbm, hbm, vmem, vmem] + [hbm] * 5,
             out_specs=(vmem, vmem, vmem, vmem),
             scratch_shapes=[
+                pltpu.VMEM((rows, dim), BF16), pltpu.VMEM((rows, dim), BF16),
                 pltpu.VMEM((cols, 2 * dim), BF16), pltpu.VMEM((ffn, dim), BF16), pltpu.VMEM((ffn, dim), BF16),
+                pltpu.VMEM((dim, 2 * pl.cdiv(ffn, 128) * 128), BF16),
                 pltpu.VMEM((ffn, dim), BF16),
-                pltpu.VMEM((rows // 2, dim), BF16), pltpu.VMEM((rows // 2, dim), BF16), pltpu.VMEM((3, chunk, dim), BF16),
+                pltpu.VMEM((rows // 2, dim), BF16), pltpu.VMEM((3, chunk, dim), BF16),
                 pltpu.VMEM((chunk, dim), BF16), pltpu.VMEM((rows, dim), BF16),
                 pltpu.VMEM((cols, rows), BF16), pltpu.VMEM((dim, rows), BF16),
-                pltpu.VMEM((4, 2 * cols, rows), F32), pltpu.VMEM((4, cols, rows), F32), pltpu.VMEM((3, cols, rows), F32),
+                pltpu.VMEM((4, 2 * cols, rows), F32), pltpu.VMEM((4, cols, rows), F32),
                 pltpu.VMEM((3, cols, rows), F32),
-                pltpu.VMEM((cols, rows), BF16), pltpu.VMEM((dim, rows), BF16),
-                pltpu.VMEM((dim, rows), F32), pltpu.VMEM((dim, rows), F32),
-                dma((4,)), dma((SLOTS,)), dma((40,)), dma((40,)),
+                pltpu.VMEM((cols, rows), BF16), pltpu.VMEM((dim, rows), BF16), pltpu.VMEM((dim, rows), F32),
+                dma((6,)), dma((SLOTS,)), dma((40,)), dma((40,)),
             ],
             compiler_params=pltpu.CompilerParams(
                 collective_id=0, has_side_effects=True, vmem_limit_bytes=int(MAIN_MIB * 1024 * 1024)),
             name="draft_main",
-        )(hidden, emb_rows, h_norm, e_norm, f_norm, o_norm,
-          proj_w.T, w_gate.T, w_up.T, w_down, head_t)
+        )(*ready, f_norm, o_norm, proj_w.T, w_gate.T, w_up.T, w_down, head_t)
 
         z, stat = pl.pallas_call(
             head_kernel,
@@ -366,11 +390,11 @@
             in_specs=[vmem, vmem, vmem, hbm],
             out_specs=(vmem, vmem),
             scratch_shapes=[
-                pltpu.VMEM((PAIR, BLOCK, dim), BF16), pltpu.VMEM((vocab % BLOCK, dim), BF16),
+                pltpu.VMEM((PAIR, BLOCK, dim), BF16), pltpu.VMEM((vocab % BLOCK, dim), BF16), pltpu.VMEM((dim, 2 * rows), BF16),
                 pltpu.VMEM((8, rows), F32), pltpu.VMEM((8, rows), F32), dma((PAIR + 1,))],
             compiler_params=pltpu.CompilerParams(vmem_limit_bytes=int(HEAD_MIB * 1024 * 1024)),
             name="head",
-        )(*(pltpu.with_memory_space_constraint(v, pltpu.VMEM) for v in (ring, o_pad, o_rows)), head_t)
+        )(*map(on_chip, (ring, o_cols, o_rows)), head_t)
 
         lse = pl.pallas_call(
             functools.partial(total_kernel, n),

time: 72.3 us -> 64.6 us (0.89)
  Pallas kernels: 70.8 us -> 63.5 us
    pallas_call x1, Pallas kernels: 11.4 us -> 4.91 us  [draft_step(): pl.pallas_call(gather_kernel, out_shape=(jax.ShapeDtypeStruct((rows, dim)...]
    pallas_call x1, Pallas kernels: 37.2 us -> 36 us  [draft_step(): pl.pallas_call(functools.partial(main_kernel, n), out_shape=(pltpu.VMEM((...]
where the time goes in v3:
time: 64.6 us; the launch traced here: 64.4 us
  Pallas kernels  63.5 us (98%)
  between operations  0.82 us (1%)
    pallas_call x1, Pallas kernels, draft_step(): pl.pallas_call(functools.partial(main_kernel, n), out_shape=(pltpu.VMEM((...  36 us
    pallas_call x1, Pallas kernels, draft_step(): pl.pallas_call(head_kernel, out_shape=(pltpu.VMEM((vocab, rows), F32), pl...  13.3 us
    pallas_call x1, Pallas kernels, draft_step(): pl.pallas_call(functools.partial(total_kernel, n), out_shape=pltpu.VMEM((...  5.23 us
    pallas_call x1, Pallas kernels, draft_step(): pl.pallas_call(gather_kernel, out_shape=(jax.ShapeDtypeStruct((rows, dim)...  4.91 us
    pallas_call x1, Pallas kernels, draft_step(): pl.pallas_call(close_kernel, out_shape=(jax.ShapeDtypeStruct((vocab, rows...  4.09 us

profile of v3, /device:TPU:0, one launch (start us, length us, event | category | flops | bytes accessed | tf_op | source)
XLA Modules:
  0.0 64.4 jit_solution(2822403551923300667)
XLA Ops:
  0.6 4.9 %gather_rows.1 = (bf16[128,1536]{1,0:T(8,128)(2,1)}, bf16[128,1536]{1,0:T(8,128)(2,1)}) custom-call(s32[128]{0:T(128)} %ids_ref.1, s32[1,128]{1,0:T(1,128)} %bitcast.11, bf16[18992,1536]{1,0:T(8,128)(2,1)} %emb_hbm.1, bf16[128,1536]{1,0:T(8,128)(2,1)} %hidden_hbm.1, f32[1536]{0:T(1024)} %h_gain.1, f32[1536]{0:T(1024)} %e_gain.1), custom_call_target="tpu_custom_call" | custom-call | tf_op jit(solution)/shard_map/gather_rows/pallas_call | solution.py:352
  5.5 36.0 %draft_main.1 = (bf16[10240,1536]{1,0:T(8,128)(2,1)S(1)}, bf16[1536,128]{1,0:T(8,128)(2,1)S(1)}, bf16[128,1536]{1,0:T(8,128)(2,1)S(1)}, bf16[1536,128]{1,0:T(8,128)(2,1)S(1)}) custom-call(bf16[128,1536]{1,0:T(8,128)(2,1)} %get-tuple-element.12.emb_hbm, bf16[128,1536]{1,0:T(8,128)(2,1)} %get-tuple-element.13.hid_hbm, f32[1536]{0:T(1024)} %f_gain.1, ...), custom_call_target="tpu_custom_call" | custom-call | tf_op jit(solution)/shard_map/draft_main/pallas_call | solution.py:363
  41.6 13.3 %head.1 = (f32[18992,128]{1,0:T(8,128)S(1)}, f32[8,128]{1,0:T(8,128)S(1)}) custom-call(bf16[10240,1536]{1,0:T(8,128)(2,1)S(1)} %get-tuple-element.14.ring, bf16[1536,128]{1,0:T(8,128)(2,1)S(1)} %get-tuple-element.15.o_in, bf16[128,1536]{1,0:T(8,128)(2,1)S(1)} %get-tuple-element.16.o_rows, bf16[18992,1536]{1,0:T(8,128)(2,1)} %bitcast.7), custom_call_target="tpu_custom_call" | custom-call | tf_op jit(solution)/shard_map/head/pallas_call | solution.py:387
  54.9 5.2 %total.1.lse_ref = f32[8,128]{1,0:T(8,128)S(1)} custom-call(f32[8,128]{1,0:T(8,128)S(1)} %get-tuple-element.18.stat_ref), custom_call_target="tpu_custom_call" | custom-call | tf_op jit(solution)/shard_map/total/pallas_call | solution.py:399
  60.1 4.1 %close.1 = (f32[18992,128]{1,0:T(8,128)}, bf16[128,1536]{1,0:T(8,128)(2,1)}) custom-call(f32[18992,128]{1,0:T(8,128)S(1)} %get-tuple-element.17.z_ref, f32[8,128]{1,0:T(8,128)S(1)} %total.1.lse_ref, bf16[1536,128]{1,0:T(8,128)(2,1)S(1)} %get-tuple-element.19.u_in), custom_call_target="tpu_custom_call" | custom-call | tf_op jit(solution)/shard_map/close/pallas_call | solution.py:409

commit v4 on v3

--- a/solution.py
+++ b/solution.py
@@ -29,8 +29,8 @@
     return lax.dot_general(a, b, (((1,), (1,)), ((), ())), preferred_element_type=F32)
 
 
-def gather_kernel(ids_ref, ids_row_ref, emb_hbm, hidden_hbm, h_gain, e_gain, emb_ref, hid_ref, buf, hid_v, sem):
-    rows, dim = emb_ref.shape
+def gather_kernel(ids_ref, ids_row_ref, emb_hbm, emb_ref, buf, sem):
+    rows = emb_ref.shape[0]
     vocab = emb_hbm.shape[0]
     base = lax.axis_index("tp") * vocab
 
@@ -38,28 +38,23 @@
         local = ids_ref[r] - base
         local = jnp.where((local >= 0) & (local < vocab), local, r * 8)
         start = pl.multiple_of((local // 8) * 8, 8)
-        pltpu.make_async_copy(emb_hbm.at[pl.ds(start, 8), :], buf.at[pl.ds(pl.multiple_of(r * 8, 8), 8), :], sem.at[0]).start()
+        pltpu.make_async_copy(emb_hbm.at[pl.ds(start, 8), :], buf.at[pl.ds(pl.multiple_of(r * 8, 8), 8), :], sem).start()
         return carry
 
     lax.fori_loop(0, rows, issue, 0, unroll=16)
-    hid_copy = pltpu.make_async_copy(hidden_hbm, hid_v, sem.at[1])
-    hid_copy.start()
     local = ids_row_ref[...] - base
     owned = (local >= 0) & (local < vocab)
     want = lax.broadcasted_iota(jnp.int32, (rows * 8, rows), 1) * 8 + (local & 7)
     here = lax.broadcasted_iota(jnp.int32, (rows * 8, rows), 0)
     pick = jnp.where((here == want) & owned, 1.0, 0.0).astype(BF16)
-    hid_copy.wait()
-    hid_ref[...] = rms(hid_v[...], h_gain[...][None, :], -1).astype(BF16)
-    pltpu.make_async_copy(emb_hbm.at[pl.ds(0, rows * 8), :], buf, sem.at[0]).wait()
-    picked = lax.dot_general(pick, buf[...], (((0,), (0,)), ((), ())), preferred_element_type=F32)
-    emb_ref[...] = rms(picked, e_gain[...][None, :], -1).astype(BF16)
-
-
-def main_kernel(n, emb_hbm, hid_hbm, f_gain, o_gain,
+    pltpu.make_async_copy(emb_hbm.at[pl.ds(0, rows * 8), :], buf, sem).wait()
+    emb_ref[...] = lax.dot_general(pick, buf[...], (((0,), (0,)), ((), ())), preferred_element_type=F32).astype(BF16)
+
+
+def main_kernel(n, emb_hbm, hid_hbm, h_hbm, e_hbm, f_hbm, o_hbm,
                 proj_hbm, gate_hbm, up_hbm, down_hbm, head_hbm,
                 ring, o_v, o_rows, u_ref,
-                emb_ref, hid_ref, proj_v, gate_v, up_v, wide_w, down_v, emb_pair, emb_in, emb_mine, emb_all, p_mine, p_all,
+                emb_ref, hid_ref, h_gain, e_gain, f_gain, o_gain, proj_v, gate_v, up_v, wide_w, down_v, emb_pair, emb_in, emb_mine, emb_all, p_mine, p_all,
                 part_v, pair_in, part_in, u_mine, u_all, wide,
                 w_sem, ring_sem, send_sem, recv_sem):
     me = lax.axis_index("tp")
@@ -73,7 +68,8 @@
     chips = (chip, chip + 1 - 2 * x, chip + 2 - 4 * y, 3 - chip)
     far = (3, 1, 2)
 
-    local = [pltpu.make_async_copy(src, dst, w_sem.at[4 + i]) for i, (src, dst) in enumerate(((emb_hbm, emb_ref), (hid_hbm, hid_ref)))]
+    local = [pltpu.make_async_copy(src, dst, w_sem.at[4 + i]) for i, (src, dst) in enumerate((
+        (emb_hbm, emb_ref), (hid_hbm, hid_ref), (h_hbm, h_gain), (e_hbm, e_gain), (f_hbm, f_gain), (o_hbm, o_gain)))]
     for copy in local:
         copy.start()
     weights = [pltpu.make_async_copy(src, dst, w_sem.at[i]) for i, (src, dst) in enumerate(
@@ -123,50 +119,63 @@
         return carry
 
     lax.fori_loop(0, SLOTS, prefetch, 0)
+    for copy in local[1:]:
+        copy.wait()
+    hid_ref[...] = rms(hid_ref[...], h_gain[...][None, :], -1).astype(BF16)
     pair.wait_recv()
     emb_sum = part(emb_ref, core, half)
     emb_sum[...] = emb_sum[...] + emb_pair[...]
     first = [send(part(emb_ref, core * (n // 2) + chips[m], chunk), emb_in.at[m - 1], chips[m] * 2 + core) for m in far]
     turned = pl.cdiv(ffn, 128) * 128
 
-    def turn(i):
-        weights[1 + i].wait()
+    def turn(i, begin, end):
         source = (gate_v, up_v)[i]
-        for at in range(0, ffn, 256):
-            size = min(256, ffn - at)
+        for at in range(begin, end, 256):
+            size = min(256, end - at)
             wide_w[:, i * turned + at:i * turned + at + size] = jnp.transpose(source[at:at + size, :])
 
     weights[0].wait()
-    local[1].wait()
     acc_h = dot_t(proj_v[:, :dim], hid_ref[...])
     wide[...] = jnp.transpose(jnp.broadcast_to(f_gain[...][None, :], (rows, dim)))
-    turn(0)
-    total = part(emb_ref, core * (n // 2) + chip, chunk)[...]
+    weights[1].wait()
+    turn(0, 0, ffn)
+    weights[2].wait()
+    total = part(emb_ref, core * (n // 2) + chip, chunk)[...].astype(F32)
     for copy in first:
         copy.wait_recv()
     for m in (0, 1, 2):
-        total = total + emb_in[m]
-    emb_mine[...] = total
-    all_gather(emb_mine, lambda j: part(emb_all, lax.rem(j, 2) * (n // 2) + lax.div(j, 2), chunk), lambda: turn(1))
+        total = total + emb_in[m].astype(F32)
+    emb_mine[...] = rms(total, e_gain[...][None, :], -1).astype(BF16)
+    all_gather(emb_mine, lambda j: part(emb_all, lax.rem(j, 2) * (n // 2) + lax.div(j, 2), chunk), lambda: turn(1, 0, 512))
     p_mine[...] = (acc_h + dot_t(proj_v[:, dim:], emb_all[...])).astype(BF16)
 
-    all_gather(p_mine, lambda j: part(p_all, j, cols))
+    all_gather(p_mine, lambda j: part(p_all, j, cols), lambda: turn(1, 512, ffn))
     normed = rms(p_all[...], wide[...], 0).astype(BF16)
     hidden = jnp.dot(jnp.transpose(normed), wide_w[...], preferred_element_type=F32)
     act = (jax.nn.silu(hidden[:, :ffn]) * hidden[:, turned:turned + ffn]).astype(BF16)
     weights[3].wait()
 
-    pairs = {}
-    for m in (3, 1, 2, 0):
-        block = jnp.dot(act, down_v[:, pl.ds(pl.multiple_of(chips[m] * 2 * cols, 2 * cols), 2 * cols)], preferred_element_type=F32)
-        part_v[m] = jnp.transpose(block)
-        pairs[m] = send(part_v.at[m, pl.ds(pl.multiple_of((1 - core) * cols, cols), cols), :], pair_in.at[m], partner)
     mine = pl.ds(pl.multiple_of(core * cols, cols), cols)
-    arriving = []
-    for m in far:
+    other = pl.ds(pl.multiple_of((1 - core) * cols, cols), cols)
+    pairs, arriving = {}, []
+
+    def narrow(m):
+        columns = pl.ds(pl.multiple_of(chips[m] * 2 * cols, 2 * cols), 2 * cols)
+        part_v[m] = jnp.transpose(jnp.dot(act, down_v[:, columns], preferred_element_type=F32))
+        pairs[m] = send(part_v.at[m, other, :], pair_in.at[m], partner)
+
+    def pass_on(m):
         pairs[m].wait_recv()
         part_v[m, mine, :] = part_v[m, mine, :] + pair_in[m]
         arriving.append(send(part_v.at[m, mine, :], part_in.at[m - 1], chips[m] * 2 + core))
+
+    narrow(3)
+    narrow(1)
+    narrow(2)
+    pass_on(3)
+    pass_on(1)
+    narrow(0)
+    pass_on(2)
     pairs[0].wait_recv()
     total = part_v[0, mine, :] + pair_in[0]
     wide[...] = jnp.transpose(jnp.broadcast_to(o_gain[...][None, :], (rows, dim)))
@@ -349,25 +358,25 @@
         hbm = pl.BlockSpec(memory_space=pl.ANY)
         dma = pltpu.SemaphoreType.DMA
         on_chip = functools.partial(pltpu.with_memory_space_constraint, memory_space=pltpu.VMEM)
-        ready = pl.pallas_call(
+        emb_rows = pl.pallas_call(
             gather_kernel,
-            out_shape=(jax.ShapeDtypeStruct((rows, dim), BF16),) * 2,
-            in_specs=[smem, vmem, hbm, hbm, vmem, vmem],
-            out_specs=(vmem, vmem),
-            scratch_shapes=[pltpu.VMEM((rows * 8, dim), BF16), pltpu.VMEM((rows, dim), BF16), dma((2,))],
+            out_shape=jax.ShapeDtypeStruct((rows, dim), BF16),
+            in_specs=[smem, vmem, hbm],
+            out_specs=vmem,
+            scratch_shapes=[pltpu.VMEM((rows * 8, dim), BF16), dma],
             compiler_params=pltpu.CompilerParams(vmem_limit_bytes=GATHER_MIB * 1024 * 1024),
             name="gather_rows",
-        )(tokens, tokens[None, :], embedding, hidden, h_norm, e_norm)
+        )(tokens, tokens[None, :], embedding)
 
         head_t = head_w.T
         ring, o_cols, o_rows, u = pl.pallas_call(
             functools.partial(main_kernel, n),
             out_shape=(pltpu.VMEM((SLOTS * BLOCK, dim), BF16), pltpu.VMEM((dim, rows), BF16), pltpu.VMEM((rows, dim), BF16),
                        pltpu.VMEM((dim, rows), BF16)),
-            in_specs=[hbm, hbm, vmem, vmem] + [hbm] * 5,
+            in_specs=[hbm] * 11,
             out_specs=(vmem, vmem, vmem, vmem),
             scratch_shapes=[
-                pltpu.VMEM((rows, dim), BF16), pltpu.VMEM((rows, dim), BF16),
+                pltpu.VMEM((rows, dim), BF16), pltpu.VMEM((rows, dim), BF16), *[pltpu.VMEM((dim,), F32)] * 4,
                 pltpu.VMEM((cols, 2 * dim), BF16), pltpu.VMEM((ffn, dim), BF16), pltpu.VMEM((ffn, dim), BF16),
                 pltpu.VMEM((dim, 2 * pl.cdiv(ffn, 128) * 128), BF16),
                 pltpu.VMEM((ffn, dim), BF16),
@@ -377,12 +386,12 @@
                 pltpu.VMEM((4, 2 * cols, rows), F32), pltpu.VMEM((4, cols, rows), F32),
                 pltpu.VMEM((3, cols, rows), F32),
                 pltpu.VMEM((cols, rows), BF16), pltpu.VMEM((dim, rows), BF16), pltpu.VMEM((dim, rows), F32),
-                dma((6,)), dma((SLOTS,)), dma((40,)), dma((40,)),
+                dma((10,)), dma((SLOTS,)), dma((40,)), dma((40,)),
             ],
             compiler_params=pltpu.CompilerParams(
                 collective_id=0, has_side_effects=True, vmem_limit_bytes=int(MAIN_MIB * 1024 * 1024)),
             name="draft_main",
-        )(*ready, f_norm, o_norm, proj_w.T, w_gate.T, w_up.T, w_down, head_t)
+        )(emb_rows, hidden, h_norm, e_norm, f_norm, o_norm, proj_w.T, w_gate.T, w_up.T, w_down, head_t)
 
         z, stat = pl.pallas_call(
             head_kernel,

time: 64.6 us -> 63.1 us (0.977)
  Pallas kernels: 63.5 us -> 62.2 us
    pallas_call x1, Pallas kernels: 4.91 us -> 4.18 us  [draft_step(): pl.pallas_call(gather_kernel, out_shape=jax.ShapeDtypeStruct((rows, dim),...]
where the time goes in v4:
time: 63.1 us; the launch traced here: 62.9 us
  Pallas kernels  62.2 us (99%)
  between operations  0.66 us (1%)
    pallas_call x1, Pallas kernels, draft_step(): pl.pallas_call(functools.partial(main_kernel, n), out_shape=(pltpu.VMEM((...  35.6 us
    pallas_call x1, Pallas kernels, draft_step(): pl.pallas_call(head_kernel, out_shape=(pltpu.VMEM((vocab, rows), F32), pl...  13.1 us
    pallas_call x1, Pallas kernels, draft_step(): pl.pallas_call(functools.partial(total_kernel, n), out_shape=pltpu.VMEM((...  5.25 us
    pallas_call x1, Pallas kernels, draft_step(): pl.pallas_call(gather_kernel, out_shape=jax.ShapeDtypeStruct((rows, dim),...  4.18 us
    pallas_call x1, Pallas kernels, draft_step(): pl.pallas_call(close_kernel, out_shape=(jax.ShapeDtypeStruct((vocab, rows...  4.09 us

profile of v4, /device:TPU:0, one launch (start us, length us, event | category | flops | bytes accessed | tf_op | source)
XLA Modules:
  0.0 62.9 jit_solution(17931901580162180786)
XLA Ops:
  0.6 4.2 %gather_rows.1.emb_hbm = bf16[128,1536]{1,0:T(8,128)(2,1)} custom-call(s32[128]{0:T(128)} %ids_ref.1, s32[1,128]{1,0:T(1,128)} %bitcast.11, bf16[18992,1536]{1,0:T(8,128)(2,1)} %emb_hbm.1), custom_call_target="tpu_custom_call" | custom-call | tf_op jit(solution)/shard_map/gather_rows/pallas_call | solution.py:361
  4.8 35.6 %draft_main.1 = (bf16[10240,1536]{1,0:T(8,128)(2,1)S(1)}, bf16[1536,128]{1,0:T(8,128)(2,1)S(1)}, bf16[128,1536]{1,0:T(8,128)(2,1)S(1)}, bf16[1536,128]{1,0:T(8,128)(2,1)S(1)}) custom-call(bf16[128,1536]{1,0:T(8,128)(2,1)} %gather_rows.1.emb_hbm, bf16[128,1536]{1,0:T(8,128)(2,1)} %hid_hbm.1, f32[1536]{0:T(1024)} %h_hbm.1, f32[1536]{0:T(1024)} %e_hbm.1, ...), custom_call_target="tpu_custom_call" | custom-call | tf_op jit(solution)/shard_map/draft_main/pallas_call | solution.py:372
  40.4 13.1 %head.1 = (f32[18992,128]{1,0:T(8,128)S(1)}, f32[8,128]{1,0:T(8,128)S(1)}) custom-call(bf16[10240,1536]{1,0:T(8,128)(2,1)S(1)} %get-tuple-element.10.ring, bf16[1536,128]{1,0:T(8,128)(2,1)S(1)} %get-tuple-element.11.o_in, bf16[128,1536]{1,0:T(8,128)(2,1)S(1)} %get-tuple-element.12.o_rows, bf16[18992,1536]{1,0:T(8,128)(2,1)} %bitcast.7), custom_call_target="tpu_custom_call" | custom-call | tf_op jit(solution)/shard_map/head/pallas_call | solution.py:396
  53.5 5.3 %total.1.lse_ref = f32[8,128]{1,0:T(8,128)S(1)} custom-call(f32[8,128]{1,0:T(8,128)S(1)} %get-tuple-element.14.stat_ref), custom_call_target="tpu_custom_call" | custom-call | tf_op jit(solution)/shard_map/total/pallas_call | solution.py:408
  58.8 4.1 %close.1 = (f32[18992,128]{1,0:T(8,128)}, bf16[128,1536]{1,0:T(8,128)(2,1)}) custom-call(f32[18992,128]{1,0:T(8,128)S(1)} %get-tuple-element.13.z_ref, f32[8,128]{1,0:T(8,128)S(1)} %total.1.lse_ref, bf16[1536,128]{1,0:T(8,128)(2,1)S(1)} %get-tuple-element.15.u_in), custom_call_target="tpu_custom_call" | custom-call | tf_op jit(solution)/shard_map/close/pallas_call | solution.py:418

commit v5 on v4

--- a/solution.py
+++ b/solution.py
@@ -59,7 +59,7 @@
                 w_sem, ring_sem, send_sem, recv_sem):
     me = lax.axis_index("tp")
     rows, dim = hid_ref.shape
-    chunk, half = rows // n, rows // 2
+    chunk = rows // n
     cols, ffn = p_mine.shape[0], gate_hbm.shape[0]
 
     core, chip = lax.rem(me, 2), lax.div(me, 2)
@@ -101,8 +101,8 @@
         return ref.at[pl.ds(pl.multiple_of(j * size, size), size), :]
 
     def all_gather(mine, place, meanwhile=lambda: None):
+        beside = [send(mine, place(me), partner)]
         arriving = {m: send(mine, place(me), chips[m] * 2 + core) for m in far}
-        beside = [send(mine, place(me), partner)]
         place(me)[...] = mine[...]
         meanwhile()
         for m in (1, 2, 3):
@@ -112,7 +112,7 @@
         for copy in beside:
             copy.wait_recv()
 
-    pair = send(part(emb_ref, 1 - core, half), emb_pair, partner)
+    pairs = {m: send(part(emb_ref, (1 - core) * (n // 2) + chips[m], chunk), emb_pair.at[m], partner) for m in (3, 2, 1, 0)}
 
     def prefetch(t, carry):
         head_copy(t).start()
@@ -122,10 +122,13 @@
     for copy in local[1:]:
         copy.wait()
     hid_ref[...] = rms(hid_ref[...], h_gain[...][None, :], -1).astype(BF16)
-    pair.wait_recv()
-    emb_sum = part(emb_ref, core, half)
-    emb_sum[...] = emb_sum[...] + emb_pair[...]
-    first = [send(part(emb_ref, core * (n // 2) + chips[m], chunk), emb_in.at[m - 1], chips[m] * 2 + core) for m in far]
+    first = []
+    for m in (3, 2, 1, 0):
+        pairs[m].wait_recv()
+        block = part(emb_ref, core * (n // 2) + chips[m], chunk)
+        block[...] = block[...] + emb_pair[m]
+        if m:
+            first.append(send(block, emb_in.at[m - 1], chips[m] * 2 + core))
     turned = pl.cdiv(ffn, 128) * 128
 
     def turn(i, begin, end):
@@ -169,13 +172,13 @@
         part_v[m, mine, :] = part_v[m, mine, :] + pair_in[m]
         arriving.append(send(part_v.at[m, mine, :], part_in.at[m - 1], chips[m] * 2 + core))
 
+    narrow(2)
     narrow(3)
     narrow(1)
-    narrow(2)
+    pass_on(2)
     pass_on(3)
+    narrow(0)
     pass_on(1)
-    narrow(0)
-    pass_on(2)
     pairs[0].wait_recv()
     total = part_v[0, mine, :] + pair_in[0]
     wide[...] = jnp.transpose(jnp.broadcast_to(o_gain[...][None, :], (rows, dim)))
@@ -380,7 +383,7 @@
                 pltpu.VMEM((cols, 2 * dim), BF16), pltpu.VMEM((ffn, dim), BF16), pltpu.VMEM((ffn, dim), BF16),
                 pltpu.VMEM((dim, 2 * pl.cdiv(ffn, 128) * 128), BF16),
                 pltpu.VMEM((ffn, dim), BF16),
-                pltpu.VMEM((rows // 2, dim), BF16), pltpu.VMEM((3, chunk, dim), BF16),
+                pltpu.VMEM((4, chunk, dim), BF16), pltpu.VMEM((3, chunk, dim), BF16),
                 pltpu.VMEM((chunk, dim), BF16), pltpu.VMEM((rows, dim), BF16),
                 pltpu.VMEM((cols, rows), BF16), pltpu.VMEM((dim, rows), BF16),
                 pltpu.VMEM((4, 2 * cols, rows), F32), pltpu.VMEM((4, cols, rows), F32),

time: 63.1 us -> 62.6 us (level)
  no operation moved by 1% of the time
where the time goes in v5:
time: 62.6 us; the launch traced here: 62.4 us
  Pallas kernels  61.7 us (99%)
  between operations  0.66 us (1%)
    pallas_call x1, Pallas kernels, draft_step(): pl.pallas_call(functools.partial(main_kernel, n), out_shape=(pltpu.VMEM((...  35.1 us
    pallas_call x1, Pallas kernels, draft_step(): pl.pallas_call(head_kernel, out_shape=(pltpu.VMEM((vocab, rows), F32), pl...  13.1 us
    pallas_call x1, Pallas kernels, draft_step(): pl.pallas_call(functools.partial(total_kernel, n), out_shape=pltpu.VMEM((...  5.25 us
    pallas_call x1, Pallas kernels, draft_step(): pl.pallas_call(gather_kernel, out_shape=jax.ShapeDtypeStruct((rows, dim),...  4.18 us
    pallas_call x1, Pallas kernels, draft_step(): pl.pallas_call(close_kernel, out_shape=(jax.ShapeDtypeStruct((vocab, rows...  4.09 us

profile of v5, /device:TPU:0, one launch (start us, length us, event | category | flops | bytes accessed | tf_op | source)
XLA Modules:
  0.0 62.4 jit_solution(5046519633432576434)
XLA Ops:
  0.6 4.2 %gather_rows.1.emb_hbm = bf16[128,1536]{1,0:T(8,128)(2,1)} custom-call(s32[128]{0:T(128)} %ids_ref.1, s32[1,128]{1,0:T(1,128)} %bitcast.11, bf16[18992,1536]{1,0:T(8,128)(2,1)} %emb_hbm.1), custom_call_target="tpu_custom_call" | custom-call | tf_op jit(solution)/shard_map/gather_rows/pallas_call | solution.py:364
  4.8 35.1 %draft_main.1 = (bf16[10240,1536]{1,0:T(8,128)(2,1)S(1)}, bf16[1536,128]{1,0:T(8,128)(2,1)S(1)}, bf16[128,1536]{1,0:T(8,128)(2,1)S(1)}, bf16[1536,128]{1,0:T(8,128)(2,1)S(1)}) custom-call(bf16[128,1536]{1,0:T(8,128)(2,1)} %gather_rows.1.emb_hbm, bf16[128,1536]{1,0:T(8,128)(2,1)} %hid_hbm.1, f32[1536]{0:T(1024)} %h_hbm.1, f32[1536]{0:T(1024)} %e_hbm.1, ...), custom_call_target="tpu_custom_call" | custom-call | tf_op jit(solution)/shard_map/draft_main/pallas_call | solution.py:375
  39.9 13.1 %head.1 = (f32[18992,128]{1,0:T(8,128)S(1)}, f32[8,128]{1,0:T(8,128)S(1)}) custom-call(bf16[10240,1536]{1,0:T(8,128)(2,1)S(1)} %get-tuple-element.10.ring, bf16[1536,128]{1,0:T(8,128)(2,1)S(1)} %get-tuple-element.11.o_in, bf16[128,1536]{1,0:T(8,128)(2,1)S(1)} %get-tuple-element.12.o_rows, bf16[18992,1536]{1,0:T(8,128)(2,1)} %bitcast.7), custom_call_target="tpu_custom_call" | custom-call | tf_op jit(solution)/shard_map/head/pallas_call | solution.py:399
  53.0 5.2 %total.1.lse_ref = f32[8,128]{1,0:T(8,128)S(1)} custom-call(f32[8,128]{1,0:T(8,128)S(1)} %get-tuple-element.14.stat_ref), custom_call_target="tpu_custom_call" | custom-call | tf_op jit(solution)/shard_map/total/pallas_call | solution.py:411
  58.3 4.1 %close.1 = (f32[18992,128]{1,0:T(8,128)}, bf16[128,1536]{1,0:T(8,128)(2,1)}) custom-call(f32[18992,128]{1,0:T(8,128)S(1)} %get-tuple-element.13.z_ref, f32[8,128]{1,0:T(8,128)S(1)} %total.1.lse_ref, bf16[1536,128]{1,0:T(8,128)(2,1)S(1)} %get-tuple-element.15.u_in), custom_call_target="tpu_custom_call" | custom-call | tf_op jit(solution)/shard_map/close/pallas_call | solution.py:421
